TPU v7x, 32 devices: a whole 2x2x4 slice. The times are simulated.
32 devices in a mesh: dp: 2 (over x), tp: 4 (over z), pp: 4 (over y, core).
Axes of the slice: x: 2, y: 2, z: 4, core: 2. Of those that a mesh axis runs over, the one named last changes fastest.
Arguments:
- x_in: bfloat16 [8, 32, 64, 2048], P(None, 'dp', 'tp'), parts along dimension 1
- ln_params: float32 [4, 4, 2048], P('pp')
- w_q: bfloat16 [4, 2048, 16, 1, 128], P('pp', None, 'tp')
- w_k: bfloat16 [4, 2048, 16, 128], P('pp', None, 'tp')
- w_v: bfloat16 [4, 2048, 16, 128], P('pp', None, 'tp')
- w_o: bfloat16 [4, 16, 1, 128, 2048], P('pp', 'tp')
- w_up: bfloat16 [4, 2048, 8192], P('pp', None, 'tp')
- w_down: bfloat16 [4, 8192, 2048], P('pp', 'tp')
Outputs:
- output: bfloat16 [4, 8, 32, 64, 2048], P('pp', None, 'dp', 'tp'), parts along dimension 2
There are 2 independent parts. A program takes and returns all parts, laid end to end along the dimension named above; an argument that names none is the same for every part.
All inputs are finite; a program needn't handle non-finite values.
Results may differ from a plain program's by a relative error of at most 0.0189104.
Values are sent between devices in bfloat16 or wider.
A program may use at most 1 GiB of HBM per device.

v0:
```python
import jax
import jax.numpy as jnp
from jax import lax
from jax.sharding import PartitionSpec as P

LN_EPS = 1e-5
ROPE_BASE = 10000.0


def layer_norm(x_act, ln_gain, ln_bias):
    x_f32 = x_act.astype(jnp.float32)
    row_mean = jnp.mean(x_f32, axis=-1, keepdims=True)
    centred = x_f32 - row_mean
    variance = jnp.mean(centred * centred, axis=-1, keepdims=True)
    return (centred * lax.rsqrt(variance + LN_EPS) * ln_gain + ln_bias).astype(jnp.bfloat16)


def rope_tables(seq_len, head_dim):
    positions = jnp.arange(seq_len, dtype=jnp.float32)
    inv_freq = ROPE_BASE ** (-2.0 * jnp.arange(head_dim // 2, dtype=jnp.float32) / head_dim)
    angles = positions[:, None] * inv_freq[None, :]
    return jnp.cos(angles), jnp.sin(angles)


def apply_rope(proj, cos_tab, sin_tab):
    half_dim = proj.shape[-1] // 2
    table_shape = (1, proj.shape[1]) + (1,) * (proj.ndim - 3) + (half_dim,)
    cos_bcast = cos_tab.reshape(table_shape)
    sin_bcast = sin_tab.reshape(table_shape)
    first_half = proj[..., :half_dim]
    second_half = proj[..., half_dim:]
    return jnp.concatenate([first_half * cos_bcast - second_half * sin_bcast, second_half * cos_bcast + first_half * sin_bcast], axis=-1)


def causal_attention(q_proj, k_proj, v_proj):
    seq_len = q_proj.shape[1]
    scores = jnp.einsum("btkgh,bskh->bktgs", q_proj, k_proj, preferred_element_type=jnp.float32) * (q_proj.shape[-1] ** -0.5)
    positions = jnp.arange(seq_len)
    allowed = positions[:, None, None] >= positions[None, None, :]
    probs_bf = jax.nn.softmax(jnp.where(allowed, scores, -1e30), axis=-1).astype(jnp.bfloat16)
    return jnp.einsum("bktgs,bskh->bktgh", probs_bf, v_proj, preferred_element_type=jnp.float32).astype(jnp.bfloat16)


def branch_partial(x_full, ln_par, w_q, w_k, w_v, w_o, w_up, w_down):
    batch_dim, seq_len, d_model = x_full.shape
    kv_local, group_size, head_dim = w_q.shape[1:]
    num_rows = batch_dim * seq_len
    h_attn = layer_norm(x_full, ln_par[0], ln_par[1]).reshape(num_rows, d_model)
    h_mlp = layer_norm(x_full, ln_par[2], ln_par[3]).reshape(num_rows, d_model)
    cos_tab, sin_tab = rope_tables(seq_len, head_dim)
    q_proj = jnp.dot(h_attn, w_q.reshape(d_model, -1), preferred_element_type=jnp.float32)
    q_proj = apply_rope(q_proj.reshape(batch_dim, seq_len, kv_local, group_size, head_dim), cos_tab, sin_tab).astype(jnp.bfloat16)
    k_proj = jnp.dot(h_attn, w_k.reshape(d_model, -1), preferred_element_type=jnp.float32)
    k_proj = apply_rope(k_proj.reshape(batch_dim, seq_len, kv_local, head_dim), cos_tab, sin_tab).astype(jnp.bfloat16)
    v_proj = jnp.dot(h_attn, w_v.reshape(d_model, -1), preferred_element_type=jnp.float32).astype(jnp.bfloat16)
    v_proj = v_proj.reshape(batch_dim, seq_len, kv_local, head_dim)
    context = causal_attention(q_proj, k_proj, v_proj)
    attn_out = jnp.einsum("bktgh,kghd->btd", context, w_o, preferred_element_type=jnp.float32)
    hidden = jax.nn.gelu(jnp.dot(h_mlp, w_up, preferred_element_type=jnp.float32), approximate=False).astype(jnp.bfloat16)
    mlp_out = jnp.dot(hidden, w_down, preferred_element_type=jnp.float32).reshape(batch_dim, seq_len, d_model)
    return (attn_out + mlp_out).astype(jnp.bfloat16)


def solution(mesh):
    pp_size = mesh.shape["pp"]
    send_pairs = [(src_idx, src_idx + 1) for src_idx in range(pp_size - 1)]

    def stage_layer(x_shard, layer_weights):
        ln_par, wq_s, wk_s, wv_s, wo_s, wup_s, wdown_s = layer_weights
        x_full = lax.all_gather(x_shard, "tp", axis=1, tiled=True)
        partial_sum = branch_partial(x_full, ln_par, wq_s, wk_s, wv_s, wo_s, wup_s, wdown_s)
        reduced = lax.psum_scatter(partial_sum, "tp", scatter_dimension=1, tiled=True)
        return (x_shard.astype(jnp.float32) + reduced.astype(jnp.float32)).astype(jnp.bfloat16)

    def stage_body(x_in, ln_params, w_q, w_k, w_v, w_o, w_up, w_down):
        stage_idx = lax.axis_index("pp")
        num_micro = x_in.shape[0]
        layer_weights = (ln_params[0], w_q[0], w_k[0], w_v[0], w_o[0], w_up[0], w_down[0])

        def micro_step(step_idx, loop_carry):
            recv_buf, out_buf = loop_carry
            first_in = lax.dynamic_index_in_dim(x_in, jnp.minimum(step_idx, num_micro - 1), axis=0, keepdims=False)
            layer_in = jnp.where(stage_idx == 0, first_in, recv_buf)
            layer_out = stage_layer(layer_in, layer_weights)
            slot_idx = step_idx - stage_idx
            is_valid = (slot_idx >= 0) & (slot_idx < num_micro)
            slot_safe = jnp.clip(slot_idx, 0, num_micro - 1)
            previous = lax.dynamic_index_in_dim(out_buf, slot_safe, axis=0, keepdims=False)
            out_buf = lax.dynamic_update_index_in_dim(out_buf, jnp.where(is_valid, layer_out, previous), slot_safe, axis=0)
            recv_buf = lax.ppermute(layer_out, "pp", send_pairs)
            return recv_buf, out_buf

        init_carry = (jnp.zeros_like(x_in[0]), jnp.zeros_like(x_in))
        _, out_buf = lax.fori_loop(0, num_micro + pp_size - 1, micro_step, init_carry)
        return out_buf[None]

    in_specs = (P(None, "dp", "tp", None), P("pp", None, None), P("pp", None, "tp", None, None), P("pp", None, "tp", None), P("pp", None, "tp", None), P("pp", "tp", None, None, None), P("pp", None, "tp"), P("pp", "tp", None))
    return jax.shard_map(stage_body, mesh=mesh, in_specs=in_specs, out_specs=P("pp", None, "dp", "tp", None), check_vma=False)
```

profile of v0, /device:TPU:1, one launch (start us, length us, event | category | flops | bytes accessed | tf_op | source)
XLA Modules:
  0.0 2862.7 jit_solution(9790516728122184505)
XLA Ops:
  19.8 2836.1 %while.17 = (s32[]{:T(128)}, bf16[16,16,2048]{2,1,0:T(8,128)(2,1)S(1)}, bf16[8,16,16,2048]{3,2,1,0:T(8,128)(2,1)}, pred[]{:T(512)}, bf16[8,16,16,2048]{3,2,1,0:T...) while((s32[]{:T(128)}, ...), condition=%wide.region_6.7_spmd, body=%wide.region_0.6_spmd.sunk | while | flops 26090153984 | bytes 203699184 | solution.py:94
  22.4 82.0 %all-gather.2.cloned.1.call-done = bf16[16,64,2048]{2,1,0:T(8,128)(2,1)} async-done(((bf16[16,16,2048]{2,1,0:T(8,128)(2,1)}), bf16[16,64,2048]{2,1,0:T(8,128)(2,1)}) %all-gather.2.cloned.1.call-update) | async-done | bytes 4194320 | tf_op jit(solution)/shard_map/while/body/eval_jaxpr/all_gather | solution.py:70
  185.7 73.5 %reduce-scatter.2.cloned.1.call-done = bf16[16,16,2048]{2,1,0:T(8,128)(2,1)} async-done(((bf16[16,64,2048]{2,1,0:T(8,128)(2,1)}), bf16[16,16,2048]{2,1,0:T(8,128)(2,1)}) %reduce-scatter.2.cloned.1.call-update) | async-done | bytes 1048592 | tf_op jit(solution)/shard_map/while/body/eval_jaxpr/reduce_scatter | solution.py:72
  280.9 81.2 %all-gather.2.cloned.1.call-done = bf16[16,64,2048]{2,1,0:T(8,128)(2,1)} async-done(((bf16[16,16,2048]{2,1,0:T(8,128)(2,1)}), bf16[16,64,2048]{2,1,0:T(8,128)(2,1)}) %all-gather.2.cloned.1.call-update) | async-done | bytes 4194320 | tf_op jit(solution)/shard_map/while/body/eval_jaxpr/all_gather | solution.py:70
  391.3 38.2 %fusion.191 = f32[1024,2048]{1,0:T(8,128)} fusion(bf16[2048,2048]{1,0:T(8,128)(2,1)} %get-tuple-element.509, bf16[1024,2048]{1,0:T(8,128)(2,1)} %bitcast.123, bf16[2048,2048]{1,0:T(8,128)(2,1)} %get-tuple-element.508), kind=kOutput, calls=%fused_computation.33.clone.1 | convolution fusion | flops 17316184064 | bytes 29360128 | tf_op jit(solution)/shard_map/while/body/eval_jaxpr/dot_general | solution.py:60
  443.5 73.5 %reduce-scatter.2.cloned.1.call-done = bf16[16,16,2048]{2,1,0:T(8,128)(2,1)} async-done(((bf16[16,64,2048]{2,1,0:T(8,128)(2,1)}), bf16[16,16,2048]{2,1,0:T(8,128)(2,1)}) %reduce-scatter.2.cloned.1.call-update) | async-done | bytes 1048592 | tf_op jit(solution)/shard_map/while/body/eval_jaxpr/reduce_scatter | solution.py:72
  538.7 81.2 %all-gather.2.cloned.1.call-done = bf16[16,64,2048]{2,1,0:T(8,128)(2,1)} async-done(((bf16[16,16,2048]{2,1,0:T(8,128)(2,1)}), bf16[16,64,2048]{2,1,0:T(8,128)(2,1)}) %all-gather.2.cloned.1.call-update) | async-done | bytes 4194320 | tf_op jit(solution)/shard_map/while/body/eval_jaxpr/all_gather | solution.py:70
  701.2 73.5 %reduce-scatter.2.cloned.1.call-done = bf16[16,16,2048]{2,1,0:T(8,128)(2,1)} async-done(((bf16[16,64,2048]{2,1,0:T(8,128)(2,1)}), bf16[16,16,2048]{2,1,0:T(8,128)(2,1)}) %reduce-scatter.2.cloned.1.call-update) | async-done | bytes 1048592 | tf_op jit(solution)/shard_map/while/body/eval_jaxpr/reduce_scatter | solution.py:72
  796.5 81.2 %all-gather.2.cloned.1.call-done = bf16[16,64,2048]{2,1,0:T(8,128)(2,1)} async-done(((bf16[16,16,2048]{2,1,0:T(8,128)(2,1)}), bf16[16,64,2048]{2,1,0:T(8,128)(2,1)}) %all-gather.2.cloned.1.call-update) | async-done | bytes 4194320 | tf_op jit(solution)/shard_map/while/body/eval_jaxpr/all_gather | solution.py:70
  959.0 73.5 %reduce-scatter.2.cloned.1.call-done = bf16[16,16,2048]{2,1,0:T(8,128)(2,1)} async-done(((bf16[16,64,2048]{2,1,0:T(8,128)(2,1)}), bf16[16,16,2048]{2,1,0:T(8,128)(2,1)}) %reduce-scatter.2.cloned.1.call-update) | async-done | bytes 1048592 | tf_op jit(solution)/shard_map/while/body/eval_jaxpr/reduce_scatter | solution.py:72
  1054.2 81.2 %all-gather.2.cloned.1.call-done = bf16[16,64,2048]{2,1,0:T(8,128)(2,1)} async-done(((bf16[16,16,2048]{2,1,0:T(8,128)(2,1)}), bf16[16,64,2048]{2,1,0:T(8,128)(2,1)}) %all-gather.2.cloned.1.call-update) | async-done | bytes 4194320 | tf_op jit(solution)/shard_map/while/body/eval_jaxpr/all_gather | solution.py:70
  1216.7 73.5 %reduce-scatter.2.cloned.1.call-done = bf16[16,16,2048]{2,1,0:T(8,128)(2,1)} async-done(((bf16[16,64,2048]{2,1,0:T(8,128)(2,1)}), bf16[16,16,2048]{2,1,0:T(8,128)(2,1)}) %reduce-scatter.2.cloned.1.call-update) | async-done | bytes 1048592 | tf_op jit(solution)/shard_map/while/body/eval_jaxpr/reduce_scatter | solution.py:72
  1312.0 81.2 %all-gather.2.cloned.1.call-done = bf16[16,64,2048]{2,1,0:T(8,128)(2,1)} async-done(((bf16[16,16,2048]{2,1,0:T(8,128)(2,1)}), bf16[16,64,2048]{2,1,0:T(8,128)(2,1)}) %all-gather.2.cloned.1.call-update) | async-done | bytes 4194320 | tf_op jit(solution)/shard_map/while/body/eval_jaxpr/all_gather | solution.py:70
  1474.5 73.5 %reduce-scatter.2.cloned.1.call-done = bf16[16,16,2048]{2,1,0:T(8,128)(2,1)} async-done(((bf16[16,64,2048]{2,1,0:T(8,128)(2,1)}), bf16[16,16,2048]{2,1,0:T(8,128)(2,1)}) %reduce-scatter.2.cloned.1.call-update) | async-done | bytes 1048592 | tf_op jit(solution)/shard_map/while/body/eval_jaxpr/reduce_scatter | solution.py:72
  1569.7 81.2 %all-gather.2.cloned.1.call-done = bf16[16,64,2048]{2,1,0:T(8,128)(2,1)} async-done(((bf16[16,16,2048]{2,1,0:T(8,128)(2,1)}), bf16[16,64,2048]{2,1,0:T(8,128)(2,1)}) %all-gather.2.cloned.1.call-update) | async-done | bytes 4194320 | tf_op jit(solution)/shard_map/while/body/eval_jaxpr/all_gather | solution.py:70
  1732.3 73.5 %reduce-scatter.2.cloned.1.call-done = bf16[16,16,2048]{2,1,0:T(8,128)(2,1)} async-done(((bf16[16,64,2048]{2,1,0:T(8,128)(2,1)}), bf16[16,16,2048]{2,1,0:T(8,128)(2,1)}) %reduce-scatter.2.cloned.1.call-update) | async-done | bytes 1048592 | tf_op jit(solution)/shard_map/while/body/eval_jaxpr/reduce_scatter | solution.py:72
  1827.5 81.2 %all-gather.2.cloned.1.call-done = bf16[16,64,2048]{2,1,0:T(8,128)(2,1)} async-done(((bf16[16,16,2048]{2,1,0:T(8,128)(2,1)}), bf16[16,64,2048]{2,1,0:T(8,128)(2,1)}) %all-gather.2.cloned.1.call-update) | async-done | bytes 4194320 | tf_op jit(solution)/shard_map/while/body/eval_jaxpr/all_gather | solution.py:70
  1990.0 73.5 %reduce-scatter.2.cloned.1.call-done = bf16[16,16,2048]{2,1,0:T(8,128)(2,1)} async-done(((bf16[16,64,2048]{2,1,0:T(8,128)(2,1)}), bf16[16,16,2048]{2,1,0:T(8,128)(2,1)}) %reduce-scatter.2.cloned.1.call-update) | async-done | bytes 1048592 | tf_op jit(solution)/shard_map/while/body/eval_jaxpr/reduce_scatter | solution.py:72
  2085.2 81.2 %all-gather.2.cloned.1.call-done = bf16[16,64,2048]{2,1,0:T(8,128)(2,1)} async-done(((bf16[16,16,2048]{2,1,0:T(8,128)(2,1)}), bf16[16,64,2048]{2,1,0:T(8,128)(2,1)}) %all-gather.2.cloned.1.call-update) | async-done | bytes 4194320 | tf_op jit(solution)/shard_map/while/body/eval_jaxpr/all_gather | solution.py:70
  2247.8 73.5 %reduce-scatter.2.cloned.1.call-done = bf16[16,16,2048]{2,1,0:T(8,128)(2,1)} async-done(((bf16[16,64,2048]{2,1,0:T(8,128)(2,1)}), bf16[16,16,2048]{2,1,0:T(8,128)(2,1)}) %reduce-scatter.2.cloned.1.call-update) | async-done | bytes 1048592 | tf_op jit(solution)/shard_map/while/body/eval_jaxpr/reduce_scatter | solution.py:72
  2343.0 81.2 %all-gather.2.cloned.1.call-done = bf16[16,64,2048]{2,1,0:T(8,128)(2,1)} async-done(((bf16[16,16,2048]{2,1,0:T(8,128)(2,1)}), bf16[16,64,2048]{2,1,0:T(8,128)(2,1)}) %all-gather.2.cloned.1.call-update) | async-done | bytes 4194320 | tf_op jit(solution)/shard_map/while/body/eval_jaxpr/all_gather | solution.py:70
  2505.5 73.5 %reduce-scatter.2.cloned.1.call-done = bf16[16,16,2048]{2,1,0:T(8,128)(2,1)} async-done(((bf16[16,64,2048]{2,1,0:T(8,128)(2,1)}), bf16[16,16,2048]{2,1,0:T(8,128)(2,1)}) %reduce-scatter.2.cloned.1.call-update) | async-done | bytes 1048592 | tf_op jit(solution)/shard_map/while/body/eval_jaxpr/reduce_scatter | solution.py:72
  2600.8 81.2 %all-gather.2.cloned.1.call-done = bf16[16,64,2048]{2,1,0:T(8,128)(2,1)} async-done(((bf16[16,16,2048]{2,1,0:T(8,128)(2,1)}), bf16[16,64,2048]{2,1,0:T(8,128)(2,1)}) %all-gather.2.cloned.1.call-update) | async-done | bytes 4194320 | tf_op jit(solution)/shard_map/while/body/eval_jaxpr/all_gather | solution.py:70
  2763.3 73.5 %reduce-scatter.2.cloned.1.call-done = bf16[16,16,2048]{2,1,0:T(8,128)(2,1)} async-done(((bf16[16,64,2048]{2,1,0:T(8,128)(2,1)}), bf16[16,16,2048]{2,1,0:T(8,128)(2,1)}) %reduce-scatter.2.cloned.1.call-update) | async-done | bytes 1048592 | tf_op jit(solution)/shard_map/while/body/eval_jaxpr/reduce_scatter | solution.py:72
  (390 shorter events, 1108.0 us)
Async XLA Ops:
  19.8 84.6 %all-gather.2.cloned.1.call-start = ((), (), s32[]{:S(2)}) async-start(), calls=%async_computation.1 | async-start | bytes 5242880 | tf_op jit(solution)/shard_map/while/body/eval_jaxpr/all_gather | solution.py:70
  22.1 237.0 %reduce-scatter.2.cloned.1.call-start = ((), (), s32[]{:S(2)}) async-start(), calls=%async_computation.2 | async-start | bytes 5242880 | tf_op jit(solution)/shard_map/while/body/eval_jaxpr/reduce_scatter | solution.py:72
  278.3 83.8 %all-gather.2.cloned.1.call-start = ((), (), s32[]{:S(2)}) async-start(), calls=%async_computation.1 | async-start | bytes 5242880 | tf_op jit(solution)/shard_map/while/body/eval_jaxpr/all_gather | solution.py:70
  280.7 236.3 %reduce-scatter.2.cloned.1.call-start = ((), (), s32[]{:S(2)}) async-start(), calls=%async_computation.2 | async-start | bytes 5242880 | tf_op jit(solution)/shard_map/while/body/eval_jaxpr/reduce_scatter | solution.py:72
  536.1 83.8 %all-gather.2.cloned.1.call-start = ((), (), s32[]{:S(2)}) async-start(), calls=%async_computation.1 | async-start | bytes 5242880 | tf_op jit(solution)/shard_map/while/body/eval_jaxpr/all_gather | solution.py:70
  538.4 236.2 %reduce-scatter.2.cloned.1.call-start = ((), (), s32[]{:S(2)}) async-start(), calls=%async_computation.2 | async-start | bytes 5242880 | tf_op jit(solution)/shard_map/while/body/eval_jaxpr/reduce_scatter | solution.py:72
  777.5 16.3 collective-permute-start
  793.8 83.8 %all-gather.2.cloned.1.call-start = ((), (), s32[]{:S(2)}) async-start(), calls=%async_computation.1 | async-start | bytes 5242880 | tf_op jit(solution)/shard_map/while/body/eval_jaxpr/all_gather | solution.py:70
  796.2 236.2 %reduce-scatter.2.cloned.1.call-start = ((), (), s32[]{:S(2)}) async-start(), calls=%async_computation.2 | async-start | bytes 5242880 | tf_op jit(solution)/shard_map/while/body/eval_jaxpr/reduce_scatter | solution.py:72
  1051.6 83.8 %all-gather.2.cloned.1.call-start = ((), (), s32[]{:S(2)}) async-start(), calls=%async_computation.1 | async-start | bytes 5242880 | tf_op jit(solution)/shard_map/while/body/eval_jaxpr/all_gather | solution.py:70
  1053.9 236.3 %reduce-scatter.2.cloned.1.call-start = ((), (), s32[]{:S(2)}) async-start(), calls=%async_computation.2 | async-start | bytes 5242880 | tf_op jit(solution)/shard_map/while/body/eval_jaxpr/reduce_scatter | solution.py:72
  1309.4 83.8 %all-gather.2.cloned.1.call-start = ((), (), s32[]{:S(2)}) async-start(), calls=%async_computation.1 | async-start | bytes 5242880 | tf_op jit(solution)/shard_map/while/body/eval_jaxpr/all_gather | solution.py:70
  1311.7 236.3 %reduce-scatter.2.cloned.1.call-start = ((), (), s32[]{:S(2)}) async-start(), calls=%async_computation.2 | async-start | bytes 5242880 | tf_op jit(solution)/shard_map/while/body/eval_jaxpr/reduce_scatter | solution.py:72
  1567.1 83.8 %all-gather.2.cloned.1.call-start = ((), (), s32[]{:S(2)}) async-start(), calls=%async_computation.1 | async-start | bytes 5242880 | tf_op jit(solution)/shard_map/while/body/eval_jaxpr/all_gather | solution.py:70
  1569.5 236.3 %reduce-scatter.2.cloned.1.call-start = ((), (), s32[]{:S(2)}) async-start(), calls=%async_computation.2 | async-start | bytes 5242880 | tf_op jit(solution)/shard_map/while/body/eval_jaxpr/reduce_scatter | solution.py:72
  1824.9 83.8 %all-gather.2.cloned.1.call-start = ((), (), s32[]{:S(2)}) async-start(), calls=%async_computation.1 | async-start | bytes 5242880 | tf_op jit(solution)/shard_map/while/body/eval_jaxpr/all_gather | solution.py:70
  1827.2 236.2 %reduce-scatter.2.cloned.1.call-start = ((), (), s32[]{:S(2)}) async-start(), calls=%async_computation.2 | async-start | bytes 5242880 | tf_op jit(solution)/shard_map/while/body/eval_jaxpr/reduce_scatter | solution.py:72
  2066.3 16.3 collective-permute-start
  2082.6 83.8 %all-gather.2.cloned.1.call-start = ((), (), s32[]{:S(2)}) async-start(), calls=%async_computation.1 | async-start | bytes 5242880 | tf_op jit(solution)/shard_map/while/body/eval_jaxpr/all_gather | solution.py:70
  2085.0 236.2 %reduce-scatter.2.cloned.1.call-start = ((), (), s32[]{:S(2)}) async-start(), calls=%async_computation.2 | async-start | bytes 5242880 | tf_op jit(solution)/shard_map/while/body/eval_jaxpr/reduce_scatter | solution.py:72
  2340.4 83.8 %all-gather.2.cloned.1.call-start = ((), (), s32[]{:S(2)}) async-start(), calls=%async_computation.1 | async-start | bytes 5242880 | tf_op jit(solution)/shard_map/while/body/eval_jaxpr/all_gather | solution.py:70
  2342.7 236.2 %reduce-scatter.2.cloned.1.call-start = ((), (), s32[]{:S(2)}) async-start(), calls=%async_computation.2 | async-start | bytes 5242880 | tf_op jit(solution)/shard_map/while/body/eval_jaxpr/reduce_scatter | solution.py:72
  2598.1 83.8 %all-gather.2.cloned.1.call-start = ((), (), s32[]{:S(2)}) async-start(), calls=%async_computation.1 | async-start | bytes 5242880 | tf_op jit(solution)/shard_map/while/body/eval_jaxpr/all_gather | solution.py:70
  2600.5 236.3 %reduce-scatter.2.cloned.1.call-start = ((), (), s32[]{:S(2)}) async-start(), calls=%async_computation.2 | async-start | bytes 5242880 | tf_op jit(solution)/shard_map/while/body/eval_jaxpr/reduce_scatter | solution.py:72
  (54 other events, 1220.2 us)
Sparse Core Ops, SparseCore 0:
  22.3 82.0 all-gather.1
  184.5 74.5 reduce-scatter.1
  280.8 81.2 all-gather.1
  442.3 74.5 reduce-scatter.1
  538.6 81.2 all-gather.1
  700.0 74.5 reduce-scatter.1
  796.3 81.2 all-gather.1
  957.8 74.5 reduce-scatter.1
  1054.1 81.2 all-gather.1
  1215.6 74.5 reduce-scatter.1
  1311.8 81.2 all-gather.1
  1473.3 74.5 reduce-scatter.1
  1569.6 81.2 all-gather.1
  1731.1 74.5 reduce-scatter.1
  1827.3 81.2 all-gather.1
  1988.8 74.5 reduce-scatter.1
  2085.1 81.2 all-gather.1
  2246.6 74.5 reduce-scatter.1
  2342.9 81.2 all-gather.1
  2504.3 74.5 reduce-scatter.1
  2600.6 81.2 all-gather.1
  2762.1 74.5 reduce-scatter.1
where the time goes:
time: 2870 us; the launch traced here: 2860 us
  waiting for transfers between devices  1830 us (64%)
  matrix products  700 us (24%)
  other arithmetic  204 us (7%)
  local copies, waits for them, and re-layouts  61.5 us (2%)
  starting transfers between devices  51.2 us (2%)
    all_gather x11, waiting for transfers between devices, stage_layer(): x_full = lax.all_gather(x_shard, 'tp', axis=1, tiled=True)  894 us
    reduce_scatter x11, waiting for transfers between devices, stage_layer(): lax.psum_scatter(partial_sum, 'tp', scatter_dimension=1, tiled=True)  808 us
    dot_general x11, matrix products, branch_partial(): jnp.dot(hidden, w_down, preferred_element_type=jnp.float32)  421 us
    ppermute x11, waiting for transfers between devices, micro_step(): recv_buf = lax.ppermute(layer_out, 'pp', send_pairs)  129 us
    dot_general x11, matrix products, branch_partial(): jnp.einsum('bktgh,kghd->btd', context, w_o, preferred_element_type=jnp.fl...  90.7 us
  transfers between devices with their start and end apart: 33, of which 33 were waited for; matrix products, arithmetic and copies ran while one was open for 1% of the time, Pallas kernels for 0%

commit v1 on v0

v1 whole, which is shorter than its diff:
```python
import functools

import jax
import jax.numpy as jnp
from jax import lax
from jax.experimental import pallas as pl
from jax.experimental.pallas import tpu as pltpu
from jax.sharding import PartitionSpec as P

LN_EPS = 1e-5
ROPE_BASE = 10000.0
CHUNKS_PER_MICRO = 4
NT = 256
NX, NR, NP, NY, NS = 4, 4, 2, 3, 4
MESH = pl.DeviceIdType.MESH


def rope_tables(seq_len, head_dim):
    positions = jnp.arange(seq_len, dtype=jnp.float32)
    inv_freq = ROPE_BASE ** (-2.0 * jnp.arange(head_dim // 2, dtype=jnp.float32) / head_dim)
    angles = positions[:, None] * inv_freq[None, :]
    return jnp.cos(angles), jnp.sin(angles)


def pipeline_kernel(dims, x_hbm, ln_ref, cos_ref, sin_ref, mask_ref, wqkv_hbm, wo_hbm, wup_hbm, wdn_hbm, out_hbm,
                    wqkv, wup, wod, xin, xfull, rbuf, part, ha, hm, qkv, act, ybuf,
                    w_sem, xin_sem, ag_ss, ag_rs, rs_ss, rs_rs, out_sem, fwd_sem):
    nc, tp, pp, heads, hd = dims
    rb, d_model = xin.shape[1:]
    rows = tp * rb
    ff = wup.shape[1]
    qd = heads * hd
    last = tp - 1
    z = lax.axis_index("tp")
    s = lax.axis_index("pp")
    has_left, has_right = z > 0, z < last
    has_prev, has_next = s > 0, s < pp - 1

    def remote(src, dst, ss, rs, to):
        return pltpu.make_async_remote_copy(src_ref=src, dst_ref=dst, send_sem=ss, recv_sem=rs, device_id=to, device_id_type=MESH)

    def neighbour(way):
        return {"tp": jnp.minimum(z + 1, last) if way == 0 else jnp.maximum(z - 1, 0)}

    def ag_copy(c, h, way):
        b = jnp.clip(z - h if way == 0 else z + h, 0, last)
        src = xin.at[c] if h == 0 else xfull.at[c % NX, b]
        return remote(src, xfull.at[c % NX, b], ag_ss.at[c % NS, way, h], ag_rs.at[c % NS, way, h], neighbour(way))

    def ag_sends(h, way):
        return has_right & (z >= h) if way == 0 else has_left & (z + h <= last)

    def ag_gets(h, way):
        return z - 1 - h >= 0 if way == 0 else z + 1 + h <= last

    def rs_copy(c, h, way):
        d = jnp.clip(z + last - h if way == 0 else z - last + h, 0, last)
        return remote(part.at[c % NP, d], rbuf.at[c % NR, way, h], rs_ss.at[c % NS, way, h], rs_rs.at[c % NS, way, h], neighbour(way))

    def rs_sends(h, way):
        return z <= h if way == 0 else last - z <= h

    def rs_sends_all(h, way):
        return rs_sends(h, way) & (has_right if way == 0 else has_left)

    def rs_gets(h, way):
        return has_left & (z - 1 <= h) if way == 0 else has_right & (last - 1 - z <= h)

    def out_copy(c):
        return pltpu.make_async_copy(ybuf.at[c % NY], out_hbm.at[c], out_sem.at[c % NY])

    def fwd_copy(c):
        return remote(ybuf.at[c % NY], xin.at[c], fwd_sem.at[c % NY], xin_sem.at[c], {"pp": jnp.minimum(s + 1, pp - 1)})

    weight_copies = [
        pltpu.make_async_copy(wqkv_hbm, wqkv, w_sem.at[0]),
        pltpu.make_async_copy(wup_hbm, wup, w_sem.at[1]),
        pltpu.make_async_copy(wo_hbm, wod.at[pl.ds(0, qd)], w_sem.at[2]),
        pltpu.make_async_copy(wdn_hbm, wod.at[pl.ds(qd, ff)], w_sem.at[3]),
    ]

    @pl.when(s == 0)
    def _():
        def load(c, carry):
            pltpu.make_async_copy(x_hbm.at[c], xin.at[c], xin_sem.at[c]).start()
            return carry
        lax.fori_loop(0, nc, load, 0)

    for copy in weight_copies:
        copy.start()

    for way, alone in ((0, z == 0), (1, z == last)):
        @pl.when(alone)
        def _(way=way):
            for k in range(NR):
                rbuf[k, way, last - 1] = jnp.zeros(rbuf.shape[3:], rbuf.dtype)

    barrier = pltpu.get_barrier_semaphore()
    for there, to in ((has_left, neighbour(1)), (has_right, neighbour(0)), (has_prev, {"pp": jnp.maximum(s - 1, 0)}), (has_next, {"pp": jnp.minimum(s + 1, pp - 1)})):
        @pl.when(there)
        def _(to=to):
            pl.semaphore_signal(barrier, inc=1, device_id=to, device_id_type=MESH)
    pl.semaphore_wait(barrier, has_left.astype(jnp.int32) + has_right.astype(jnp.int32) + has_prev.astype(jnp.int32) + has_next.astype(jnp.int32))

    def on(cond, fn):
        pl.when(cond)(fn)

    def ag_start(c):
        pltpu.make_async_copy(x_hbm.at[c], xin.at[c], xin_sem.at[c]).wait()
        for way in (0, 1):
            on(ag_sends(0, way), ag_copy(c, 0, way).start)
        xfull[c % NX, z] = xin[c]

    def ag_hop(c, h):
        for way in (0, 1):
            on(ag_gets(h - 1, way), ag_copy(c, h - 1, way).wait_recv)
            if h < last:
                on(ag_sends(h, way), ag_copy(c, h, way).start)

    def ag_drain(c):
        for h in range(last):
            for way in (0, 1):
                on(ag_sends(h, way), ag_copy(c, h, way).wait_send)

    def rs_hop(c, h):
        for way in (0, 1):
            @pl.when(rs_sends_all(h, way))
            def _(way=way):
                if h > 0:
                    @pl.when(rs_gets(h - 1, way))
                    def _():
                        rs_copy(c, h - 1, way).wait_recv()
                        d = z + last - h if way == 0 else z - last + h
                        mine = part[c % NP, d].astype(jnp.float32)
                        part[c % NP, d] = (mine + rbuf[c % NR, way, h - 1].astype(jnp.float32)).astype(part.dtype)
                rs_copy(c, h, way).start()

    def rs_drain(c):
        for h in range(last):
            for way in (0, 1):
                on(rs_sends_all(h, way), rs_copy(c, h, way).wait_send)

    def finish(c):
        @pl.when(c >= NY)
        def _():
            out_copy(c - NY).wait()
            on(has_next, fwd_copy(c - NY).wait_send)
        for way in (0, 1):
            on(rs_gets(last - 1, way), rs_copy(c, last - 1, way).wait_recv)
        f32 = jnp.float32
        total = xin[c].astype(f32) + part[c % NP, z].astype(f32)
        total = total + rbuf[c % NR, 0, last - 1].astype(f32) + rbuf[c % NR, 1, last - 1].astype(f32)
        ybuf[c % NY] = total.astype(ybuf.dtype)
        on(has_next, fwd_copy(c).start)
        out_copy(c).start()

    lt = min(rb, 32)
    per_block = rb // lt

    def norms(c):
        def tile(t, carry):
            x_f32 = xfull[c % NX, t // per_block, pl.ds((t % per_block) * lt, lt)].astype(jnp.float32)
            row_mean = jnp.mean(x_f32, axis=-1, keepdims=True)
            centred = x_f32 - row_mean
            variance = jnp.mean(centred * centred, axis=-1, keepdims=True)
            unit = centred * lax.rsqrt(variance + LN_EPS)
            at = pl.ds(pl.multiple_of(t * lt, lt), lt)
            ha[at] = (unit * ln_ref[0:1] + ln_ref[1:2]).astype(ha.dtype)
            hm[at] = (unit * ln_ref[2:3] + ln_ref[3:4]).astype(hm.dtype)
            return carry
        lax.fori_loop(0, rows // lt, tile, 0, unroll=2)

    def cols(n):
        return pl.ds(pl.multiple_of(n * NT, NT), NT)

    per_tile = NT // hd

    def projections():
        def rotated(n, carry):
            y = jnp.dot(ha[...], wqkv[:, cols(n)], preferred_element_type=jnp.float32)
            for j in range(per_tile):
                head = y[:, j * hd:(j + 1) * hd]
                turned = head * cos_ref[...] + pltpu.roll(head, hd // 2, 1) * sin_ref[...]
                qkv[n * per_tile + j] = turned.astype(qkv.dtype)
            return carry
        lax.fori_loop(0, 2 * qd // NT, rotated, 0, unroll=2)

        def plain(n, carry):
            y = jnp.dot(ha[...], wqkv[:, cols(n)], preferred_element_type=jnp.float32)
            for j in range(per_tile):
                qkv[n * per_tile + j] = y[:, j * hd:(j + 1) * hd].astype(qkv.dtype)
            return carry
        lax.fori_loop(2 * qd // NT, 3 * qd // NT, plain, 0, unroll=True)

    def attention():
        for h in range(heads):
            scores = lax.dot_general(qkv[h], qkv[heads + h], (((1,), (1,)), ((), ())), preferred_element_type=jnp.float32) * (hd ** -0.5)
            floor = mask_ref[...]
            scores = jnp.where(floor == 0.0, scores, floor)
            raised = jnp.exp(scores - jnp.max(scores, axis=-1, keepdims=True))
            probs = (raised * (1.0 / jnp.sum(raised, axis=-1, keepdims=True))).astype(qkv.dtype)
            act[:, h * hd:(h + 1) * hd] = jnp.dot(probs, qkv[2 * heads + h], preferred_element_type=jnp.float32).astype(act.dtype)

    def mlp_up():
        def tile(n, carry):
            u = jnp.dot(hm[...], wup[:, cols(n)], preferred_element_type=jnp.float32)
            g = 0.5 * u * (1.0 + lax.erf(u * (0.5 ** 0.5)))
            act[:, pl.ds(pl.multiple_of(qd + n * NT, NT), NT)] = g.astype(act.dtype)
            return carry
        lax.fori_loop(0, ff // NT, tile, 0, unroll=2)

    def project_out(c):
        def tile(n, carry):
            o = jnp.dot(act[...], wod[:, cols(n)], preferred_element_type=jnp.float32).astype(part.dtype)
            for b in range(tp):
                part[c % NP, b, :, cols(n)] = o[b * rb:(b + 1) * rb]
            return carry
        lax.fori_loop(0, d_model // NT, tile, 0, unroll=2)

    def holds(c):
        return (c >= 0) & (c < nc)

    def slot(i, carry):
        @pl.when(holds(i))
        def _():
            ag_start(i)

        @pl.when(holds(i - 1))
        def _():
            ag_hop(i - 1, 2)

        @pl.when(holds(i - 4))
        def _():
            rs_drain(i - 4)

        @pl.when(holds(i - 2))
        def _():
            @pl.when(i == 2)
            def _():
                weight_copies[2].wait()
                weight_copies[3].wait()
            project_out(i - 2)
            rs_hop(i - 2, 0)

        @pl.when(holds(i - 3))
        def _():
            rs_hop(i - 3, 2)

        @pl.when(holds(i))
        def _():
            ag_hop(i, 1)

        @pl.when(holds(i - 1))
        def _():
            ag_hop(i - 1, 3)
            @pl.when(i == 1)
            def _():
                weight_copies[0].wait()
            norms(i - 1)
            projections()
            attention()

        @pl.when(holds(i - 2))
        def _():
            rs_hop(i - 2, 1)

        @pl.when(holds(i - 3))
        def _():
            finish(i - 3)

        @pl.when(holds(i - 2))
        def _():
            ag_drain(i - 2)

        @pl.when(holds(i - 1))
        def _():
            @pl.when(i == 1)
            def _():
                weight_copies[1].wait()
            mlp_up()
        return carry

    lax.fori_loop(0, nc + 4, slot, 0)

    for c in range(nc - NY, nc):
        out_copy(c).wait()
        on(has_next, fwd_copy(c).wait_send)


def solution(mesh):
    tp, pp = mesh.shape["tp"], mesh.shape["pp"]

    def stage_body(x_in, ln_params, w_q, w_k, w_v, w_o, w_up, w_down):
        num_micro, batch_dim, tok, d_model = x_in.shape
        heads, hd = w_k.shape[2:]
        ff = w_up.shape[2]
        seqs = batch_dim // CHUNKS_PER_MICRO
        nc = num_micro * CHUNKS_PER_MICRO
        rb = seqs * tok
        rows = tp * rb
        qd = heads * hd
        bf16, f32 = jnp.bfloat16, jnp.float32

        row = jnp.arange(rows)
        pos = row // rb * tok + row % tok
        seq = row % rb // tok
        cos_tab, sin_tab = rope_tables(tp * tok, hd)
        cos_rows = jnp.concatenate([cos_tab, cos_tab], axis=-1)[pos]
        sin_rows = jnp.concatenate([-sin_tab, sin_tab], axis=-1)[pos]
        same = seq[:, None] == seq[None, :]
        allowed = same & (pos[:, None] >= pos[None, :])
        mask = jnp.where(allowed, 0.0, jnp.where(same, -1e30, -3e38)).astype(f32)
        w_qkv = jnp.concatenate([w_q.reshape(d_model, qd), w_k.reshape(d_model, qd), w_v.reshape(d_model, qd)], axis=1)

        any_spec = pl.BlockSpec(memory_space=pl.ANY)
        vmem_spec = pl.BlockSpec(memory_space=pltpu.VMEM)
        dma = pltpu.SemaphoreType.DMA
        flops = 2 * num_micro * tp * batch_dim * tok * (3 * qd * d_model + qd * d_model + 2 * ff * d_model)
        out = pl.pallas_call(
            functools.partial(pipeline_kernel, (nc, tp, pp, heads, hd)),
            out_shape=jax.ShapeDtypeStruct((nc, rb, d_model), bf16),
            in_specs=[any_spec, vmem_spec, vmem_spec, vmem_spec, vmem_spec, any_spec, any_spec, any_spec, any_spec],
            out_specs=any_spec,
            scratch_shapes=[
                pltpu.VMEM((d_model, 3 * qd), bf16),
                pltpu.VMEM((d_model, ff), bf16),
                pltpu.VMEM((qd + ff, d_model), bf16),
                pltpu.VMEM((nc, rb, d_model), bf16),
                pltpu.VMEM((NX, tp, rb, d_model), bf16),
                pltpu.VMEM((NR, 2, tp - 1, rb, d_model), bf16),
                pltpu.VMEM((NP, tp, rb, d_model), bf16),
                pltpu.VMEM((rows, d_model), bf16),
                pltpu.VMEM((rows, d_model), bf16),
                pltpu.VMEM((3 * heads, rows, hd), bf16),
                pltpu.VMEM((rows, qd + ff), bf16),
                pltpu.VMEM((NY, rb, d_model), bf16),
                dma((4,)),
                dma((nc,)),
                dma((NS, 2, tp - 1)),
                dma((NS, 2, tp - 1)),
                dma((NS, 2, tp - 1)),
                dma((NS, 2, tp - 1)),
                dma((NY,)),
                dma((NY,)),
            ],
            compiler_params=pltpu.CompilerParams(collective_id=0, has_side_effects=True, vmem_limit_bytes=67043328),
            cost_estimate=pl.CostEstimate(flops=flops, bytes_accessed=50 * 2 ** 20, transcendentals=0),
            name="pipeline",
        )(x_in.reshape(nc, rb, d_model), ln_params[0], cos_rows, sin_rows, mask, w_qkv, w_o.reshape(qd, d_model), w_up[0], w_down[0])
        return out.reshape(1, num_micro, batch_dim, tok, d_model)

    in_specs = (P(None, "dp", "tp", None), P("pp", None, None), P("pp", None, "tp", None, None), P("pp", None, "tp", None), P("pp", None, "tp", None), P("pp", "tp", None, None, None), P("pp", None, "tp"), P("pp", "tp", None))
    return jax.shard_map(stage_body, mesh=mesh, in_specs=in_specs, out_specs=P("pp", None, "dp", "tp", None), check_vma=False)
```

time: 2870 us -> 990 us (0.34)
  the two profiles are of different devices: /device:TPU:1 before, /device:TPU:7 now
where the time goes in v1:
time: 990 us
  Pallas kernels  970 us (98%)
  local copies, waits for them, and re-layouts  15.4 us (2%)
    pallas_call x1, Pallas kernels, stage_body(): pl.pallas_call(functools.partial(pipeline_kernel, (nc, tp, pp, heads, hd)...  970 us

profile of v1, /device:TPU:7, one launch (start us, length us, event | category | flops | bytes accessed | tf_op | source)
XLA Modules:
  0.0 989.7 jit_solution(3037623689245208543)
XLA Ops:
  0.0 0.0 copy-start
  0.1 0.1 fusion.3
  0.2 0.1 pad_maximum_fusion.1
  0.3 1.3 gather_fusion
  1.6 1.4 gather_fusion.1
  3.0 0.9 fusion.mask_ref
  3.8 2.0 copy.15
  5.8 0.0 copy-done
  5.8 2.3 copy_bitcast_fusion
  8.1 3.0 pad_maximum_fusion.wqkv_hbm
  11.1 970.1 %pipeline.1 = bf16[32,64,2048]{2,1,0:T(8,128)(2,1)} custom-call(bf16[32,64,2048]{2,1,0:T(8,128)(2,1)} %bitcast.27, f32[4,2048]{1,0:T(4,128)} %bitcast.31, f32[256,128]{1,0:T(8,128)} %gather_fusion, f32[256,128]{1,0:T(8,128)} %gather_fusion.1, f32[256,256]{1,0:T(8,128)} %fusion.mask_ref, bf16[2048,1536]{1,0:T(8,128)(2,1)} %pad_maximum_fusion.wqkv_hbm, ...), custom_call_target="tpu_custom_call" | custom-call | flops 206158430208 | bytes 52428800 | tf_op jit(solution)/shard_map/pipeline/pallas_call | solution.py:319
  981.2 8.4 copy.17
  (4 shorter events, 0.0 us)
Async XLA Ops:
  0.0 5.8 copy-start

commit v2 on v1

--- a/solution.py
+++ b/solution.py
@@ -9,9 +9,10 @@
 
 LN_EPS = 1e-5
 ROPE_BASE = 10000.0
-CHUNKS_PER_MICRO = 4
+CHUNKS_PER_MICRO = 8
 NT = 256
-NX, NR, NP, NY, NS = 4, 4, 2, 3, 4
+NX, NR, NP, NS = 4, 4, 3, 4
+TURN = (("gather0", 0), ("scatter1", 3), ("gather2", 1), ("up", 2), ("finish", 4), ("out", 2), ("gather1", 0), ("scatter0", 2), ("scatter2", 3), ("heads", 1))
 MESH = pl.DeviceIdType.MESH
 
 
@@ -22,10 +23,10 @@
     return jnp.cos(angles), jnp.sin(angles)
 
 
-def pipeline_kernel(dims, x_hbm, ln_ref, cos_ref, sin_ref, mask_ref, wqkv_hbm, wo_hbm, wup_hbm, wdn_hbm, out_hbm,
-                    wqkv, wup, wod, xin, xfull, rbuf, part, ha, hm, qkv, act, ybuf,
-                    w_sem, xin_sem, ag_ss, ag_rs, rs_ss, rs_rs, out_sem, fwd_sem):
-    nc, tp, pp, heads, hd = dims
+def pipeline_kernel(dims, x_hbm, ln_ref, cos_ref, sin_ref, wq_hbm, wk_hbm, wv_hbm, wo_hbm, wup_hbm, wdn_hbm, xin,
+                    wqkv, wup, wod, xfull, rbuf, part, ha, hm, qkv, act, mask_ref,
+                    w_sem, xin_sem, ag_ss, ag_rs, rs_ss, rs_rs, fwd_sem):
+    nc, tp, pp, heads, hd, tok = dims
     rb, d_model = xin.shape[1:]
     rows = tp * rb
     ff = wup.shape[1]
@@ -66,17 +67,16 @@
     def rs_gets(h, way):
         return has_left & (z - 1 <= h) if way == 0 else has_right & (last - 1 - z <= h)
 
-    def out_copy(c):
-        return pltpu.make_async_copy(ybuf.at[c % NY], out_hbm.at[c], out_sem.at[c % NY])
-
     def fwd_copy(c):
-        return remote(ybuf.at[c % NY], xin.at[c], fwd_sem.at[c % NY], xin_sem.at[c], {"pp": jnp.minimum(s + 1, pp - 1)})
+        return remote(xin.at[c], xin.at[c], fwd_sem.at[c], xin_sem.at[c], {"pp": jnp.minimum(s + 1, pp - 1)})
 
     weight_copies = [
-        pltpu.make_async_copy(wqkv_hbm, wqkv, w_sem.at[0]),
-        pltpu.make_async_copy(wup_hbm, wup, w_sem.at[1]),
-        pltpu.make_async_copy(wo_hbm, wod.at[pl.ds(0, qd)], w_sem.at[2]),
-        pltpu.make_async_copy(wdn_hbm, wod.at[pl.ds(qd, ff)], w_sem.at[3]),
+        pltpu.make_async_copy(wq_hbm, wqkv.at[:, pl.ds(0, qd)], w_sem.at[0]),
+        pltpu.make_async_copy(wk_hbm, wqkv.at[:, pl.ds(qd, qd)], w_sem.at[1]),
+        pltpu.make_async_copy(wv_hbm, wqkv.at[:, pl.ds(2 * qd, qd)], w_sem.at[2]),
+        pltpu.make_async_copy(wup_hbm, wup, w_sem.at[3]),
+        pltpu.make_async_copy(wo_hbm, wod.at[pl.ds(0, qd)], w_sem.at[4]),
+        pltpu.make_async_copy(wdn_hbm, wod.at[pl.ds(qd, ff)], w_sem.at[5]),
     ]
 
     @pl.when(s == 0)
@@ -94,6 +94,12 @@
         def _(way=way):
             for k in range(NR):
                 rbuf[k, way, last - 1] = jnp.zeros(rbuf.shape[3:], rbuf.dtype)
+
+    row = lax.broadcasted_iota(jnp.int32, (rows, rows), 0)
+    col = lax.broadcasted_iota(jnp.int32, (rows, rows), 1)
+    same = row % rb // tok == col % rb // tok
+    later = row // rb * tok + row % tok >= col // rb * tok + col % tok
+    mask_ref[...] = jnp.where(same, jnp.where(later, 0.0, -1e30), -3e38)
 
     barrier = pltpu.get_barrier_semaphore()
     for there, to in ((has_left, neighbour(1)), (has_right, neighbour(0)), (has_prev, {"pp": jnp.maximum(s - 1, 0)}), (has_next, {"pp": jnp.minimum(s + 1, pp - 1)})):
@@ -141,18 +147,13 @@
                 on(rs_sends_all(h, way), rs_copy(c, h, way).wait_send)
 
     def finish(c):
-        @pl.when(c >= NY)
-        def _():
-            out_copy(c - NY).wait()
-            on(has_next, fwd_copy(c - NY).wait_send)
         for way in (0, 1):
             on(rs_gets(last - 1, way), rs_copy(c, last - 1, way).wait_recv)
         f32 = jnp.float32
         total = xin[c].astype(f32) + part[c % NP, z].astype(f32)
         total = total + rbuf[c % NR, 0, last - 1].astype(f32) + rbuf[c % NR, 1, last - 1].astype(f32)
-        ybuf[c % NY] = total.astype(ybuf.dtype)
+        xin[c] = total.astype(xin.dtype)
         on(has_next, fwd_copy(c).start)
-        out_copy(c).start()
 
     lt = min(rb, 32)
     per_block = rb // lt
@@ -220,71 +221,59 @@
     def holds(c):
         return (c >= 0) & (c < nc)
 
-    def slot(i, carry):
-        @pl.when(holds(i))
+    def weights_ready(c, first, count):
+        @pl.when(c == 0)
         def _():
-            ag_start(i)
-
-        @pl.when(holds(i - 1))
-        def _():
-            ag_hop(i - 1, 2)
-
-        @pl.when(holds(i - 4))
-        def _():
-            rs_drain(i - 4)
-
-        @pl.when(holds(i - 2))
-        def _():
-            @pl.when(i == 2)
-            def _():
-                weight_copies[2].wait()
-                weight_copies[3].wait()
-            project_out(i - 2)
-            rs_hop(i - 2, 0)
-
-        @pl.when(holds(i - 3))
-        def _():
-            rs_hop(i - 3, 2)
-
-        @pl.when(holds(i))
-        def _():
-            ag_hop(i, 1)
-
-        @pl.when(holds(i - 1))
-        def _():
-            ag_hop(i - 1, 3)
-            @pl.when(i == 1)
-            def _():
-                weight_copies[0].wait()
-            norms(i - 1)
-            projections()
-            attention()
-
-        @pl.when(holds(i - 2))
-        def _():
-            rs_hop(i - 2, 1)
-
-        @pl.when(holds(i - 3))
-        def _():
-            finish(i - 3)
-
-        @pl.when(holds(i - 2))
-        def _():
-            ag_drain(i - 2)
-
-        @pl.when(holds(i - 1))
-        def _():
-            @pl.when(i == 1)
-            def _():
-                weight_copies[1].wait()
-            mlp_up()
+            for copy in weight_copies[first:first + count]:
+                copy.wait()
+
+    def heads_step(c):
+        ag_hop(c, last)
+        weights_ready(c, 0, 3)
+        norms(c)
+        projections()
+        attention()
+
+    def up_step(c):
+        weights_ready(c, 3, 1)
+        mlp_up()
+
+    def out_step(c):
+        weights_ready(c, 4, 2)
+        ag_drain(c)
+        on(c >= NP, lambda: rs_drain(c - NP))
+        project_out(c)
+
+    steps = {
+        "gather0": ag_start,
+        "gather1": lambda c: ag_hop(c, 1),
+        "gather2": lambda c: ag_hop(c, 2),
+        "heads": heads_step,
+        "up": up_step,
+        "out": out_step,
+        "scatter0": lambda c: rs_hop(c, 0),
+        "scatter1": lambda c: rs_hop(c, 1),
+        "scatter2": lambda c: rs_hop(c, 2),
+        "finish": finish,
+    }
+
+    def turn(i, carry):
+        for name, behind in TURN:
+            c = i - behind
+            on((c >= 0) & (c < nc), functools.partial(steps[name], c))
         return carry
 
-    lax.fori_loop(0, nc + 4, slot, 0)
-
-    for c in range(nc - NY, nc):
-        out_copy(c).wait()
-        on(has_next, fwd_copy(c).wait_send)
+    lax.fori_loop(0, nc + max(behind for _, behind in TURN), turn, 0)
+
+    for c in range(nc - NP, nc):
+        rs_drain(c)
+
+    @pl.when(has_next)
+    def _():
+        def sent(c, carry):
+            fwd_copy(c).wait_send()
+            return carry
+        lax.fori_loop(0, nc, sent, 0)
 
 
 def solution(mesh):
@@ -301,31 +290,24 @@
         qd = heads * hd
         bf16, f32 = jnp.bfloat16, jnp.float32
 
-        row = jnp.arange(rows)
-        pos = row // rb * tok + row % tok
-        seq = row % rb // tok
         cos_tab, sin_tab = rope_tables(tp * tok, hd)
-        cos_rows = jnp.concatenate([cos_tab, cos_tab], axis=-1)[pos]
-        sin_rows = jnp.concatenate([-sin_tab, sin_tab], axis=-1)[pos]
-        same = seq[:, None] == seq[None, :]
-        allowed = same & (pos[:, None] >= pos[None, :])
-        mask = jnp.where(allowed, 0.0, jnp.where(same, -1e30, -3e38)).astype(f32)
-        w_qkv = jnp.concatenate([w_q.reshape(d_model, qd), w_k.reshape(d_model, qd), w_v.reshape(d_model, qd)], axis=1)
+        per_row = lambda t: jnp.broadcast_to(t.reshape(tp, 1, tok, hd), (tp, seqs, tok, hd)).reshape(rows, hd)
+        cos_rows = per_row(jnp.concatenate([cos_tab, cos_tab], axis=-1))
+        sin_rows = per_row(jnp.concatenate([-sin_tab, sin_tab], axis=-1))
 
         any_spec = pl.BlockSpec(memory_space=pl.ANY)
         vmem_spec = pl.BlockSpec(memory_space=pltpu.VMEM)
         dma = pltpu.SemaphoreType.DMA
         flops = 2 * num_micro * tp * batch_dim * tok * (3 * qd * d_model + qd * d_model + 2 * ff * d_model)
         out = pl.pallas_call(
-            functools.partial(pipeline_kernel, (nc, tp, pp, heads, hd)),
-            out_shape=jax.ShapeDtypeStruct((nc, rb, d_model), bf16),
-            in_specs=[any_spec, vmem_spec, vmem_spec, vmem_spec, vmem_spec, any_spec, any_spec, any_spec, any_spec],
-            out_specs=any_spec,
+            functools.partial(pipeline_kernel, (nc, tp, pp, heads, hd, tok)),
+            out_shape=pltpu.VMEM((nc, rb, d_model), bf16),
+            in_specs=[any_spec, vmem_spec, vmem_spec, vmem_spec] + [any_spec] * 6,
+            out_specs=vmem_spec,
             scratch_shapes=[
                 pltpu.VMEM((d_model, 3 * qd), bf16),
                 pltpu.VMEM((d_model, ff), bf16),
                 pltpu.VMEM((qd + ff, d_model), bf16),
-                pltpu.VMEM((nc, rb, d_model), bf16),
                 pltpu.VMEM((NX, tp, rb, d_model), bf16),
                 pltpu.VMEM((NR, 2, tp - 1, rb, d_model), bf16),
                 pltpu.VMEM((NP, tp, rb, d_model), bf16),
@@ -333,20 +315,19 @@
                 pltpu.VMEM((rows, d_model), bf16),
                 pltpu.VMEM((3 * heads, rows, hd), bf16),
                 pltpu.VMEM((rows, qd + ff), bf16),
-                pltpu.VMEM((NY, rb, d_model), bf16),
-                dma((4,)),
+                pltpu.VMEM((rows, rows), f32),
+                dma((6,)),
                 dma((nc,)),
                 dma((NS, 2, tp - 1)),
                 dma((NS, 2, tp - 1)),
                 dma((NS, 2, tp - 1)),
                 dma((NS, 2, tp - 1)),
-                dma((NY,)),
-                dma((NY,)),
+                dma((nc,)),
             ],
-            compiler_params=pltpu.CompilerParams(collective_id=0, has_side_effects=True, vmem_limit_bytes=67043328),
+            compiler_params=pltpu.CompilerParams(collective_id=0, has_side_effects=True, vmem_limit_bytes=52 * 2 ** 20),
             cost_estimate=pl.CostEstimate(flops=flops, bytes_accessed=50 * 2 ** 20, transcendentals=0),
             name="pipeline",
-        )(x_in.reshape(nc, rb, d_model), ln_params[0], cos_rows, sin_rows, mask, w_qkv, w_o.reshape(qd, d_model), w_up[0], w_down[0])
+        )(x_in.reshape(nc, rb, d_model), ln_params[0], cos_rows, sin_rows, w_q.reshape(d_model, qd), w_k.reshape(d_model, qd), w_v.reshape(d_model, qd), w_o.reshape(qd, d_model), w_up[0], w_down[0])
         return out.reshape(1, num_micro, batch_dim, tok, d_model)
 
     in_specs = (P(None, "dp", "tp", None), P("pp", None, None), P("pp", None, "tp", None, None), P("pp", None, "tp", None), P("pp", None, "tp", None), P("pp", "tp", None, None, None), P("pp", None, "tp"), P("pp", "tp", None))

time: 990 us -> 878 us (0.89)
  the two profiles are of different devices: /device:TPU:7 before, /device:TPU:5 now
where the time goes in v2:
time: 878 us; the launch traced here: 877 us
  Pallas kernels  866 us (99%)
  local copies, waits for them, and re-layouts  10.8 us (1%)
    pallas_call x1, Pallas kernels, stage_body(): pl.pallas_call(functools.partial(pipeline_kernel, (nc, tp, pp, heads, hd,...  866 us

profile of v2, /device:TPU:5, one launch (start us, length us, event | category | flops | bytes accessed | tf_op | source)
XLA Modules:
  0.0 877.4 jit_solution(845949265220914910)
XLA Ops:
  0.0 0.2 fusion
  0.2 0.1 maximum_bitcast_fusion
  0.3 0.6 broadcast_in_dim.17
  1.0 0.6 broadcast_in_dim.19
  1.6 0.0 copy-start
  1.6 0.0 copy-start.1
  1.6 3.4 copy.15
  5.0 0.0 copy-done
  5.0 0.0 copy-done.1
  5.0 2.8 copy_bitcast_fusion
  7.8 866.3 %pipeline.1 = bf16[64,32,2048]{2,1,0:T(8,128)(2,1)S(1)} custom-call(bf16[64,32,2048]{2,1,0:T(8,128)(2,1)} %bitcast.33, f32[4,2048]{1,0:T(4,128)} %bitcast.37, f32[128,128]{1,0:T(8,128)} %bitcast.31, f32[128,128]{1,0:T(8,128)} %bitcast.32, bf16[2048,512]{1,0:T(8,128)(2,1)} %bitcast.28, bf16[2048,512]{1,0:T(8,128)(2,1)} %get-tuple-element.11.wk_hbm, ...), custom_call_target="tpu_custom_call" | custom-call | flops 206158430208 | bytes 52428800 | tf_op jit(solution)/shard_map/pipeline/pallas_call | solution.py:302
  874.0 3.4 copy.17
  (2 shorter events, 0.0 us)
Async XLA Ops:
  1.6 3.4 copy-start
  1.6 3.4 copy-start.1

commit v3 on v2

--- a/solution.py
+++ b/solution.py
@@ -12,6 +12,7 @@
 CHUNKS_PER_MICRO = 8
 NT = 256
 NX, NR, NP, NS = 4, 4, 3, 4
+LATE = 3
 TURN = (("gather0", 0), ("scatter1", 3), ("gather2", 1), ("up", 2), ("finish", 4), ("out", 2), ("gather1", 0), ("scatter0", 2), ("scatter2", 3), ("heads", 1))
 MESH = pl.DeviceIdType.MESH
 
@@ -23,10 +24,11 @@
     return jnp.cos(angles), jnp.sin(angles)
 
 
-def pipeline_kernel(dims, x_hbm, ln_ref, cos_ref, sin_ref, wq_hbm, wk_hbm, wv_hbm, wo_hbm, wup_hbm, wdn_hbm, xin,
-                    wqkv, wup, wod, xfull, rbuf, part, ha, hm, qkv, act, mask_ref,
-                    w_sem, xin_sem, ag_ss, ag_rs, rs_ss, rs_rs, fwd_sem):
-    nc, tp, pp, heads, hd, tok = dims
+def pipeline_kernel(dims, x_hbm, cos_tab, sin_tab, wq_hbm, wk_hbm, wv_hbm, ln_hbm, wup_hbm, wo_hbm, wdn_hbm,
+                    xin, lq_hbm, lk_hbm, lv_hbm, lln_hbm, lup_hbm, lo_hbm, ldn_hbm,
+                    wqkv, ln_ref, wup, wod, xlate, xfull, rbuf, part, ha, hm, qkv, act, mask_ref, cos_ref, sin_ref,
+                    w_sem, xin_sem, ag_ss, ag_rs, rs_ss, rs_rs, fwd_sem, home_sem, lw_ss, lw_rs):
+    nc, nl, tp, pp, heads, hd, tok = dims
     rb, d_model = xin.shape[1:]
     rows = tp * rb
     ff = wup.shape[1]
@@ -36,6 +38,8 @@
     s = lax.axis_index("pp")
     has_left, has_right = z > 0, z < last
     has_prev, has_next = s > 0, s < pp - 1
+    half = pp // 2
+    front = s < half
 
     def remote(src, dst, ss, rs, to):
         return pltpu.make_async_remote_copy(src_ref=src, dst_ref=dst, send_sem=ss, recv_sem=rs, device_id=to, device_id_type=MESH)
@@ -43,9 +47,9 @@
     def neighbour(way):
         return {"tp": jnp.minimum(z + 1, last) if way == 0 else jnp.maximum(z - 1, 0)}
 
-    def ag_copy(c, h, way):
+    def ag_copy(c, h, way, first=None):
         b = jnp.clip(z - h if way == 0 else z + h, 0, last)
-        src = xin.at[c] if h == 0 else xfull.at[c % NX, b]
+        src = (first if first is not None else xin.at[0]) if h == 0 else xfull.at[c % NX, b]
         return remote(src, xfull.at[c % NX, b], ag_ss.at[c % NS, way, h], ag_rs.at[c % NS, way, h], neighbour(way))
 
     def ag_sends(h, way):
@@ -67,17 +71,24 @@
     def rs_gets(h, way):
         return has_left & (z - 1 <= h) if way == 0 else has_right & (last - 1 - z <= h)
 
-    def fwd_copy(c):
-        return remote(xin.at[c], xin.at[c], fwd_sem.at[c], xin_sem.at[c], {"pp": jnp.minimum(s + 1, pp - 1)})
-
-    weight_copies = [
-        pltpu.make_async_copy(wq_hbm, wqkv.at[:, pl.ds(0, qd)], w_sem.at[0]),
-        pltpu.make_async_copy(wk_hbm, wqkv.at[:, pl.ds(qd, qd)], w_sem.at[1]),
-        pltpu.make_async_copy(wv_hbm, wqkv.at[:, pl.ds(2 * qd, qd)], w_sem.at[2]),
-        pltpu.make_async_copy(wup_hbm, wup, w_sem.at[3]),
-        pltpu.make_async_copy(wo_hbm, wod.at[pl.ds(0, qd)], w_sem.at[4]),
-        pltpu.make_async_copy(wdn_hbm, wod.at[pl.ds(qd, ff)], w_sem.at[5]),
-    ]
+    def fwd_copy(v):
+        return remote(xin.at[v], xin.at[v], fwd_sem.at[v], xin_sem.at[v], {"pp": jnp.minimum(s + 1, pp - 1)})
+
+    def turn_copy(v):
+        return remote(xin.at[v], xlate.at[v - (nc - nl)], fwd_sem.at[v], xin_sem.at[v + nl], {"pp": 0})
+
+    def next_late_copy(v):
+        return remote(xlate.at[v - nc], xlate.at[v - nc], fwd_sem.at[v], xin_sem.at[v], {"pp": jnp.minimum(s + 1, pp - 1)})
+
+    def home_copy(v):
+        return remote(xlate.at[v - nc], xin.at[v - nl], home_sem.at[v - nc], xin_sem.at[v - nl], {"pp": jnp.minimum(s + half, pp - 1)})
+
+    own = [wq_hbm, wk_hbm, wv_hbm, ln_hbm, wup_hbm, wo_hbm, wdn_hbm]
+    late = [lq_hbm, lk_hbm, lv_hbm, lln_hbm, lup_hbm, lo_hbm, ldn_hbm]
+    held = [wqkv.at[:, pl.ds(0, qd)], wqkv.at[:, pl.ds(qd, qd)], wqkv.at[:, pl.ds(2 * qd, qd)], ln_ref, wup, wod.at[pl.ds(0, qd)], wod.at[pl.ds(qd, ff)]]
+    weight_copies = [pltpu.make_async_copy(src, dst, w_sem.at[k]) for k, (src, dst) in enumerate(zip(own, held))]
+    swap_copies = [pltpu.make_async_copy(src, dst, w_sem.at[k]) for k, (src, dst) in enumerate(zip(late, held))]
+    lend_copies = [remote(src, dst, lw_ss.at[k], lw_rs.at[k], {"pp": jnp.maximum(s - half, 0)}) for k, (src, dst) in enumerate(zip(own, late))]
 
     @pl.when(s == 0)
     def _():
@@ -100,22 +111,39 @@
     same = row % rb // tok == col % rb // tok
     later = row // rb * tok + row % tok >= col // rb * tok + col % tok
     mask_ref[...] = jnp.where(same, jnp.where(later, 0.0, -1e30), -3e38)
+    for b in range(tp):
+        for q in range(rb // tok):
+            to, of = slice(b * rb + q * tok, b * rb + (q + 1) * tok), slice(b * tok, (b + 1) * tok)
+            cos_ref[to] = cos_tab[of]
+            sin_ref[to] = sin_tab[of]
 
     barrier = pltpu.get_barrier_semaphore()
-    for there, to in ((has_left, neighbour(1)), (has_right, neighbour(0)), (has_prev, {"pp": jnp.maximum(s - 1, 0)}), (has_next, {"pp": jnp.minimum(s + 1, pp - 1)})):
+    for there, to in ((has_left, neighbour(1)), (has_right, neighbour(0)), (has_prev, {"pp": jnp.maximum(s - 1, 0)}), (has_next, {"pp": jnp.minimum(s + 1, pp - 1)}), (front, {"pp": jnp.minimum(s + half, pp - 1)}), (s >= half, {"pp": jnp.maximum(s - half, 0)})):
         @pl.when(there)
         def _(to=to):
             pl.semaphore_signal(barrier, inc=1, device_id=to, device_id_type=MESH)
-    pl.semaphore_wait(barrier, has_left.astype(jnp.int32) + has_right.astype(jnp.int32) + has_prev.astype(jnp.int32) + has_next.astype(jnp.int32))
+    pl.semaphore_wait(barrier, has_left.astype(jnp.int32) + has_right.astype(jnp.int32) + has_prev.astype(jnp.int32) + has_next.astype(jnp.int32) + 1)
+
+    @pl.when(s >= half)
+    def _():
+        for copy in lend_copies:
+            copy.start()
 
     def on(cond, fn):
         pl.when(cond)(fn)
 
+    def in_its_place(c, fn):
+        on(c < nc, lambda: fn(xin.at[c]))
+        on(c >= nc, lambda: fn(xlate.at[c - nc]))
+
     def ag_start(c):
-        pltpu.make_async_copy(x_hbm.at[c], xin.at[c], xin_sem.at[c]).wait()
-        for way in (0, 1):
-            on(ag_sends(0, way), ag_copy(c, 0, way).start)
-        xfull[c % NX, z] = xin[c]
+        pltpu.make_async_copy(x_hbm.at[0], xin.at[0], xin_sem.at[c]).wait()
+
+        def send(place):
+            for way in (0, 1):
+                on(ag_sends(0, way), ag_copy(c, 0, way, place).start)
+            xfull[c % NX, z] = place[...]
+        in_its_place(c, send)
 
     def ag_hop(c, h):
         for way in (0, 1):
@@ -150,10 +178,17 @@
         for way in (0, 1):
             on(rs_gets(last - 1, way), rs_copy(c, last - 1, way).wait_recv)
         f32 = jnp.float32
-        total = xin[c].astype(f32) + part[c % NP, z].astype(f32)
-        total = total + rbuf[c % NR, 0, last - 1].astype(f32) + rbuf[c % NR, 1, last - 1].astype(f32)
-        xin[c] = total.astype(xin.dtype)
-        on(has_next, fwd_copy(c).start)
+
+        def add(place):
+            total = place[...].astype(f32) + part[c % NP, z].astype(f32)
+            total = total + rbuf[c % NR, 0, last - 1].astype(f32) + rbuf[c % NR, 1, last - 1].astype(f32)
+            place[...] = total.astype(xin.dtype)
+        in_its_place(c, add)
+        turns = (s == half - 1) & (c >= nc - nl)
+        on(has_next & (c < nc) & ~turns, lambda: fwd_copy(c).start())
+        on(turns & (c < nc), lambda: turn_copy(c).start())
+        on((s < half - 1) & (c >= nc), lambda: next_late_copy(c).start())
+        on(front & (c >= nc), lambda: home_copy(c).start())
 
     lt = min(rb, 32)
     per_block = rb // lt
@@ -221,59 +256,89 @@
     def holds(c):
         return (c >= 0) & (c < nc)
 
-    def weights_ready(c, first, count):
-        @pl.when(c == 0)
+    def weights_ready(c, ks):
+        @pl.when((c == 0) | (c == nc))
         def _():
-            for copy in weight_copies[first:first + count]:
-                copy.wait()
-
-    def heads_step(c):
+            for k in ks:
+                weight_copies[k].wait()
+
+    def swap_weights(c, ks):
+        @pl.when(front & (c == nc - 1))
+        def _():
+            for k in ks:
+                lend_copies[k].wait_recv()
+                swap_copies[k].start()
+
+    def heads_step(c, lo):
         ag_hop(c, last)
-        weights_ready(c, 0, 3)
+        weights_ready(c, (0, 1, 2, 3))
         norms(c)
         projections()
+        swap_weights(c, (0, 1, 2, 3))
         attention()
 
-    def up_step(c):
-        weights_ready(c, 3, 1)
+    def up_step(c, lo):
+        weights_ready(c, (4,))
         mlp_up()
-
-    def out_step(c):
-        weights_ready(c, 4, 2)
+        swap_weights(c, (4,))
+
+    def out_step(c, lo):
+        weights_ready(c, (5, 6))
         ag_drain(c)
-        on(c >= NP, lambda: rs_drain(c - NP))
+        on(c - NP >= lo, lambda: rs_drain(c - NP))
         project_out(c)
+        swap_weights(c, (5, 6))
 
     steps = {
-        "gather0": ag_start,
-        "gather1": lambda c: ag_hop(c, 1),
-        "gather2": lambda c: ag_hop(c, 2),
+        "gather0": lambda c, lo: ag_start(c),
+        "gather1": lambda c, lo: ag_hop(c, 1),
+        "gather2": lambda c, lo: ag_hop(c, 2),
         "heads": heads_step,
         "up": up_step,
         "out": out_step,
-        "scatter0": lambda c: rs_hop(c, 0),
-        "scatter1": lambda c: rs_hop(c, 1),
-        "scatter2": lambda c: rs_hop(c, 2),
-        "finish": finish,
+        "scatter0": lambda c, lo: rs_hop(c, 0),
+        "scatter1": lambda c, lo: rs_hop(c, 1),
+        "scatter2": lambda c, lo: rs_hop(c, 2),
+        "finish": lambda c, lo: finish(c),
     }
-
-    def turn(i, carry):
-        for name, behind in TURN:
-            c = i - behind
-            on((c >= 0) & (c < nc), functools.partial(steps[name], c))
+    span = max(behind for _, behind in TURN)
+
+    def segment(k, carry):
+        lo = k * nc
+        hi = jnp.where(front, jnp.where(k == 0, nc, nc + nl), jnp.where(k == 0, nc - nl, nc))
+
+        def turn(i, carry):
+            for name, behind in TURN:
+                c = i - behind
+                on((c >= lo) & (c < hi), functools.partial(steps[name], c, lo))
+            return carry
+
+        lax.fori_loop(lo, jnp.where(hi > lo, hi + span, lo), turn, 0)
+        for back in range(1, NP + 1):
+            on(hi - back >= lo, lambda: rs_drain(hi - back))
         return carry
 
-    lax.fori_loop(0, nc + max(behind for _, behind in TURN), turn, 0)
-
-    for c in range(nc - NP, nc):
-        rs_drain(c)
+    lax.fori_loop(0, 2, segment, 0)
 
     @pl.when(has_next)
     def _():
-        def sent(c, carry):
-            fwd_copy(c).wait_send()
-            return carry
-        lax.fori_loop(0, nc, sent, 0)
+        def sent(v, carry):
+            fwd_copy(v).wait_send()
+            return carry
+        lax.fori_loop(0, jnp.where(s < half - 1, nc, nc - nl), sent, 0)
+
+    for k in range(nl):
+        on(s == half - 1, turn_copy(nc - nl + k).wait_send)
+        on(s < half - 1, next_late_copy(nc + k).wait_send)
+        on(front, home_copy(nc + k).wait_send)
+
+    @pl.when(s >= half)
+    def _():
+        for copy in lend_copies:
+            copy.wait_send()
+        for k in range(nl):
+            c = nc - nl + k
+            pltpu.make_async_copy(x_hbm.at[0], xin.at[0], xin_sem.at[c]).wait()
 
 
 def solution(mesh):
@@ -291,23 +356,26 @@
         bf16, f32 = jnp.bfloat16, jnp.float32
 
         cos_tab, sin_tab = rope_tables(tp * tok, hd)
-        per_row = lambda t: jnp.broadcast_to(t.reshape(tp, 1, tok, hd), (tp, seqs, tok, hd)).reshape(rows, hd)
-        cos_rows = per_row(jnp.concatenate([cos_tab, cos_tab], axis=-1))
-        sin_rows = per_row(jnp.concatenate([-sin_tab, sin_tab], axis=-1))
+        cos_full = jnp.concatenate([cos_tab, cos_tab], axis=-1)
+        sin_full = jnp.concatenate([-sin_tab, sin_tab], axis=-1)
 
         any_spec = pl.BlockSpec(memory_space=pl.ANY)
         vmem_spec = pl.BlockSpec(memory_space=pltpu.VMEM)
         dma = pltpu.SemaphoreType.DMA
         flops = 2 * num_micro * tp * batch_dim * tok * (3 * qd * d_model + qd * d_model + 2 * ff * d_model)
-        out = pl.pallas_call(
-            functools.partial(pipeline_kernel, (nc, tp, pp, heads, hd, tok)),
-            out_shape=pltpu.VMEM((nc, rb, d_model), bf16),
-            in_specs=[any_spec, vmem_spec, vmem_spec, vmem_spec] + [any_spec] * 6,
-            out_specs=vmem_spec,
+        out, *_ = pl.pallas_call(
+            functools.partial(pipeline_kernel, (nc, LATE, tp, pp, heads, hd, tok)),
+            out_shape=[pltpu.VMEM((nc, rb, d_model), bf16)] + [jax.ShapeDtypeStruct((d_model, qd), bf16)] * 3 + [
+                jax.ShapeDtypeStruct((4, d_model), f32), jax.ShapeDtypeStruct((d_model, ff), bf16),
+                jax.ShapeDtypeStruct((qd, d_model), bf16), jax.ShapeDtypeStruct((ff, d_model), bf16)],
+            in_specs=[any_spec, vmem_spec, vmem_spec] + [any_spec] * 7,
+            out_specs=[vmem_spec] + [any_spec] * 7,
             scratch_shapes=[
                 pltpu.VMEM((d_model, 3 * qd), bf16),
+                pltpu.VMEM((4, d_model), f32),
                 pltpu.VMEM((d_model, ff), bf16),
                 pltpu.VMEM((qd + ff, d_model), bf16),
+                pltpu.VMEM((LATE, rb, d_model), bf16),
                 pltpu.VMEM((NX, tp, rb, d_model), bf16),
                 pltpu.VMEM((NR, 2, tp - 1, rb, d_model), bf16),
                 pltpu.VMEM((NP, tp, rb, d_model), bf16),
@@ -316,18 +384,23 @@
                 pltpu.VMEM((3 * heads, rows, hd), bf16),
                 pltpu.VMEM((rows, qd + ff), bf16),
                 pltpu.VMEM((rows, rows), f32),
-                dma((6,)),
-                dma((nc,)),
+                pltpu.VMEM((rows, hd), f32),
+                pltpu.VMEM((rows, hd), f32),
+                dma((7,)),
+                dma((nc + LATE,)),
                 dma((NS, 2, tp - 1)),
                 dma((NS, 2, tp - 1)),
                 dma((NS, 2, tp - 1)),
                 dma((NS, 2, tp - 1)),
-                dma((nc,)),
+                dma((nc + LATE,)),
+                dma((LATE,)),
+                dma((7,)),
+                dma((7,)),
             ],
             compiler_params=pltpu.CompilerParams(collective_id=0, has_side_effects=True, vmem_limit_bytes=52 * 2 ** 20),
             cost_estimate=pl.CostEstimate(flops=flops, bytes_accessed=50 * 2 ** 20, transcendentals=0),
             name="pipeline",
-        )(x_in.reshape(nc, rb, d_model), ln_params[0], cos_rows, sin_rows, w_q.reshape(d_model, qd), w_k.reshape(d_model, qd), w_v.reshape(d_model, qd), w_o.reshape(qd, d_model), w_up[0], w_down[0])
+        )(x_in.reshape(nc, rb, d_model), cos_full, sin_full, w_q.reshape(d_model, qd), w_k.reshape(d_model, qd), w_v.reshape(d_model, qd), ln_params[0], w_up[0], w_o.reshape(qd, d_model), w_down[0])
         return out.reshape(1, num_micro, batch_dim, tok, d_model)
 
     in_specs = (P(None, "dp", "tp", None), P("pp", None, None), P("pp", None, "tp", None, None), P("pp", None, "tp", None), P("pp", None, "tp", None), P("pp", "tp", None, None, None), P("pp", None, "tp"), P("pp", "tp", None))

time: 878 us -> 857 us (0.976)
  the two profiles are of different devices: /device:TPU:5 before, /device:TPU:1 now
where the time goes in v3:
time: 857 us
  Pallas kernels  846 us (99%)
  local copies, waits for them, and re-layouts  9.57 us (1%)
    pallas_call x1, Pallas kernels, stage_body(): pl.pallas_call(functools.partial(pipeline_kernel, (nc, LATE, tp, pp, head...  846 us

profile of v3, /device:TPU:1, one launch (start us, length us, event | category | flops | bytes accessed | tf_op | source)
XLA Modules:
  0.0 856.6 jit_solution(12071381492888147131)
XLA Ops:
  0.0 0.1 fusion.2
  0.2 0.7 pad_maximum_fusion
  0.9 0.0 copy-start
  0.9 0.0 copy-start.1
  0.9 3.4 copy.15
  4.3 0.0 copy-done
  4.3 0.0 copy-done.1
  4.3 2.7 copy_bitcast_fusion
  7.1 846.1 %pipeline.1 = (bf16[64,32,2048]{2,1,0:T(8,128)(2,1)S(1)}, bf16[2048,512]{1,0:T(8,128)(2,1)}, bf16[2048,512]{1,0:T(8,128)(2,1)}, bf16[2048,512]{1,0:T(8,128)(2,1)...) custom-call(bf16[64,32,2048]{2,1,0:T(8,128)(2,1)} %bitcast.25, ...), custom_call_target="tpu_custom_call" | custom-call | flops 206158430208 | bytes 52428800 | tf_op jit(solution)/shard_map/pipeline/pallas_call | solution.py:366
  853.2 3.4 copy.17
  (1 shorter events, 0.0 us)
Async XLA Ops:
  0.9 3.4 copy-start
  0.9 3.4 copy-start.1

commit v4 on v3

--- a/solution.py
+++ b/solution.py
@@ -13,7 +13,8 @@
 NT = 256
 NX, NR, NP, NS = 4, 4, 3, 4
 LATE = 3
-TURN = (("gather0", 0), ("scatter1", 3), ("gather2", 1), ("up", 2), ("finish", 4), ("out", 2), ("gather1", 0), ("scatter0", 2), ("scatter2", 3), ("heads", 1))
+AHEAD = 4
+TURN = (("gather0", 0), ("scatter1", 3), ("gather2", 1), ("up", 2), ("finish", 4), ("out", 2), ("scatter0", 2), ("gather1", 0), ("arrive", 1), ("scatter2", 3), ("heads", 1))
 MESH = pl.DeviceIdType.MESH
 
 
@@ -41,6 +42,9 @@
     half = pp // 2
     front = s < half
 
+    def on(cond, fn):
+        pl.when(cond)(fn)
+
     def remote(src, dst, ss, rs, to):
         return pltpu.make_async_remote_copy(src_ref=src, dst_ref=dst, send_sem=ss, recv_sem=rs, device_id=to, device_id_type=MESH)
 
@@ -90,13 +94,17 @@
     swap_copies = [pltpu.make_async_copy(src, dst, w_sem.at[k]) for k, (src, dst) in enumerate(zip(late, held))]
     lend_copies = [remote(src, dst, lw_ss.at[k], lw_rs.at[k], {"pp": jnp.maximum(s - half, 0)}) for k, (src, dst) in enumerate(zip(own, late))]
 
-    @pl.when(s == 0)
-    def _():
-        def load(c, carry):
-            pltpu.make_async_copy(x_hbm.at[c], xin.at[c], xin_sem.at[c]).start()
-            return carry
-        lax.fori_loop(0, nc, load, 0)
-
+    barrier = pltpu.get_barrier_semaphore()
+    for there, to in ((has_left, neighbour(1)), (has_right, neighbour(0)), (has_prev, {"pp": jnp.maximum(s - 1, 0)}), (has_next, {"pp": jnp.minimum(s + 1, pp - 1)}), (front, {"pp": jnp.minimum(s + half, pp - 1)}), (s >= half, {"pp": jnp.maximum(s - half, 0)})):
+        @pl.when(there)
+        def _(to=to):
+            pl.semaphore_signal(barrier, inc=1, device_id=to, device_id_type=MESH)
+
+    def load(c):
+        return pltpu.make_async_copy(x_hbm.at[c], xin.at[c], xin_sem.at[c])
+
+    for c in range(AHEAD):
+        on(s == 0, load(c).start)
     for copy in weight_copies:
         copy.start()
 
@@ -117,11 +125,6 @@
             cos_ref[to] = cos_tab[of]
             sin_ref[to] = sin_tab[of]
 
-    barrier = pltpu.get_barrier_semaphore()
-    for there, to in ((has_left, neighbour(1)), (has_right, neighbour(0)), (has_prev, {"pp": jnp.maximum(s - 1, 0)}), (has_next, {"pp": jnp.minimum(s + 1, pp - 1)}), (front, {"pp": jnp.minimum(s + half, pp - 1)}), (s >= half, {"pp": jnp.maximum(s - half, 0)})):
-        @pl.when(there)
-        def _(to=to):
-            pl.semaphore_signal(barrier, inc=1, device_id=to, device_id_type=MESH)
     pl.semaphore_wait(barrier, has_left.astype(jnp.int32) + has_right.astype(jnp.int32) + has_prev.astype(jnp.int32) + has_next.astype(jnp.int32) + 1)
 
     @pl.when(s >= half)
@@ -129,14 +132,12 @@
         for copy in lend_copies:
             copy.start()
 
-    def on(cond, fn):
-        pl.when(cond)(fn)
-
     def in_its_place(c, fn):
         on(c < nc, lambda: fn(xin.at[c]))
         on(c >= nc, lambda: fn(xlate.at[c - nc]))
 
     def ag_start(c):
+        on((s == 0) & (c + AHEAD < nc), lambda: load(c + AHEAD).start())
         pltpu.make_async_copy(x_hbm.at[0], xin.at[0], xin_sem.at[c]).wait()
 
         def send(place):
@@ -270,7 +271,6 @@
                 swap_copies[k].start()
 
     def heads_step(c, lo):
-        ag_hop(c, last)
         weights_ready(c, (0, 1, 2, 3))
         norms(c)
         projections()
@@ -293,6 +293,7 @@
         "gather0": lambda c, lo: ag_start(c),
         "gather1": lambda c, lo: ag_hop(c, 1),
         "gather2": lambda c, lo: ag_hop(c, 2),
+        "arrive": lambda c, lo: ag_hop(c, last),
         "heads": heads_step,
         "up": up_step,
         "out": out_step,

time: 857 us -> 858 us (level)
  no operation moved by 1% of the time
where the time goes in v4:
time: 858 us
  Pallas kernels  847 us (99%)
  local copies, waits for them, and re-layouts  9.57 us (1%)
    pallas_call x1, Pallas kernels, stage_body(): pl.pallas_call(functools.partial(pipeline_kernel, (nc, LATE, tp, pp, head...  847 us

profile of v4, /device:TPU:1, one launch (start us, length us, event | category | flops | bytes accessed | tf_op | source)
XLA Modules:
  0.0 857.8 jit_solution(9947331573801011626)
XLA Ops:
  0.0 0.1 fusion.2
  0.2 0.7 pad_maximum_fusion
  0.9 0.0 copy-start
  0.9 0.0 copy-start.1
  0.9 3.4 copy.15
  4.3 0.0 copy-done
  4.3 0.0 copy-done.1
  4.3 2.7 copy_bitcast_fusion
  7.1 847.3 %pipeline.1 = (bf16[64,32,2048]{2,1,0:T(8,128)(2,1)S(1)}, bf16[2048,512]{1,0:T(8,128)(2,1)}, bf16[2048,512]{1,0:T(8,128)(2,1)}, bf16[2048,512]{1,0:T(8,128)(2,1)...) custom-call(bf16[64,32,2048]{2,1,0:T(8,128)(2,1)} %bitcast.25, ...), custom_call_target="tpu_custom_call" | custom-call | flops 206158430208 | bytes 52428800 | tf_op jit(solution)/shard_map/pipeline/pallas_call | solution.py:367
  854.4 3.4 copy.17
  (1 shorter events, 0.0 us)
Async XLA Ops:
  0.9 3.4 copy-start
  0.9 3.4 copy-start.1

commit v5 on v4

--- a/solution.py
+++ b/solution.py
@@ -14,7 +14,7 @@
 NX, NR, NP, NS = 4, 4, 3, 4
 LATE = 3
 AHEAD = 4
-TURN = (("gather0", 0), ("scatter1", 3), ("gather2", 1), ("up", 2), ("finish", 4), ("out", 2), ("scatter0", 2), ("gather1", 0), ("arrive", 1), ("scatter2", 3), ("heads", 1))
+TURN = (("gather0", 0), ("scatter1", 3), ("gather2", 1), ("up", 2), ("finish", 4), ("out", 2), ("scatter0", 2), ("lay_q", 0), ("gather1", 0), ("lay_k", 0), ("lay_v", 1), ("arrive", 1), ("scatter2", 3), ("heads", 1))
 MESH = pl.DeviceIdType.MESH
 
 
@@ -27,7 +27,7 @@
 
 def pipeline_kernel(dims, x_hbm, cos_tab, sin_tab, wq_hbm, wk_hbm, wv_hbm, ln_hbm, wup_hbm, wo_hbm, wdn_hbm,
                     xin, lq_hbm, lk_hbm, lv_hbm, lln_hbm, lup_hbm, lo_hbm, ldn_hbm,
-                    wqkv, ln_ref, wup, wod, xlate, xfull, rbuf, part, ha, hm, qkv, act, mask_ref, cos_ref, sin_ref,
+                    raw, wqkv, ln_ref, wup, wod, xlate, xfull, rbuf, part, ha, hm, qkv, act, mask_ref, cos_ref, sin_ref,
                     w_sem, xin_sem, ag_ss, ag_rs, rs_ss, rs_rs, fwd_sem, home_sem, lw_ss, lw_rs):
     nc, nl, tp, pp, heads, hd, tok = dims
     rb, d_model = xin.shape[1:]
@@ -90,9 +90,9 @@
     own = [wq_hbm, wk_hbm, wv_hbm, ln_hbm, wup_hbm, wo_hbm, wdn_hbm]
     late = [lq_hbm, lk_hbm, lv_hbm, lln_hbm, lup_hbm, lo_hbm, ldn_hbm]
     held = [wqkv.at[:, pl.ds(0, qd)], wqkv.at[:, pl.ds(qd, qd)], wqkv.at[:, pl.ds(2 * qd, qd)], ln_ref, wup, wod.at[pl.ds(0, qd)], wod.at[pl.ds(qd, ff)]]
-    weight_copies = [pltpu.make_async_copy(src, dst, w_sem.at[k]) for k, (src, dst) in enumerate(zip(own, held))]
+    weight_copies = [pltpu.make_async_copy(src, dst, w_sem.at[k]) for k, (src, dst) in enumerate(zip(own, [raw.at[0], raw.at[1], raw.at[2]] + held[3:]))]
     swap_copies = [pltpu.make_async_copy(src, dst, w_sem.at[k]) for k, (src, dst) in enumerate(zip(late, held))]
-    lend_copies = [remote(src, dst, lw_ss.at[k], lw_rs.at[k], {"pp": jnp.maximum(s - half, 0)}) for k, (src, dst) in enumerate(zip(own, late))]
+    lend_copies = [remote(src, dst, lw_ss.at[k], lw_rs.at[k], {"pp": jnp.maximum(s - half, 0)}) for k, (src, dst) in enumerate(zip(held[:3] + own[3:], late))]
 
     barrier = pltpu.get_barrier_semaphore()
     for there, to in ((has_left, neighbour(1)), (has_right, neighbour(0)), (has_prev, {"pp": jnp.maximum(s - 1, 0)}), (has_next, {"pp": jnp.minimum(s + 1, pp - 1)}), (front, {"pp": jnp.minimum(s + half, pp - 1)}), (s >= half, {"pp": jnp.maximum(s - half, 0)})):
@@ -107,6 +107,22 @@
         on(s == 0, load(c).start)
     for copy in weight_copies:
         copy.start()
+
+    lay_rows = 64
+
+    def lay(k):
+        weight_copies[k].wait()
+
+        def some(t, carry):
+            at = pl.ds(pl.multiple_of(t * lay_rows, lay_rows), lay_rows)
+            wqkv[at, k * qd:(k + 1) * qd] = raw[k, at].reshape(lay_rows, qd)
+            return carry
+        lax.fori_loop(0, d_model // lay_rows, some, 0)
+
+    @pl.when(s > 0)
+    def _():
+        for k in range(3):
+            lay(k)
 
     for way, alone in ((0, z == 0), (1, z == last)):
         @pl.when(alone)
@@ -271,7 +287,11 @@
                 swap_copies[k].start()
 
     def heads_step(c, lo):
-        weights_ready(c, (0, 1, 2, 3))
+        @pl.when(c == nc)
+        def _():
+            for k in range(3):
+                swap_copies[k].wait()
+        weights_ready(c, (3,))
         norms(c)
         projections()
         swap_weights(c, (0, 1, 2, 3))
@@ -293,6 +313,9 @@
         "gather0": lambda c, lo: ag_start(c),
         "gather1": lambda c, lo: ag_hop(c, 1),
         "gather2": lambda c, lo: ag_hop(c, 2),
+        "lay_q": lambda c, lo: on((s == 0) & (c == 0), lambda: lay(0)),
+        "lay_k": lambda c, lo: on((s == 0) & (c == 0), lambda: lay(1)),
+        "lay_v": lambda c, lo: on((s == 0) & (c == 0), lambda: lay(2)),
         "arrive": lambda c, lo: ag_hop(c, last),
         "heads": heads_step,
         "up": up_step,
@@ -372,6 +395,7 @@
             in_specs=[any_spec, vmem_spec, vmem_spec] + [any_spec] * 7,
             out_specs=[vmem_spec] + [any_spec] * 7,
             scratch_shapes=[
+                pltpu.VMEM((3, d_model, heads, hd), bf16),
                 pltpu.VMEM((d_model, 3 * qd), bf16),
                 pltpu.VMEM((4, d_model), f32),
                 pltpu.VMEM((d_model, ff), bf16),
@@ -401,7 +425,7 @@
             compiler_params=pltpu.CompilerParams(collective_id=0, has_side_effects=True, vmem_limit_bytes=52 * 2 ** 20),
             cost_estimate=pl.CostEstimate(flops=flops, bytes_accessed=50 * 2 ** 20, transcendentals=0),
             name="pipeline",
-        )(x_in.reshape(nc, rb, d_model), cos_full, sin_full, w_q.reshape(d_model, qd), w_k.reshape(d_model, qd), w_v.reshape(d_model, qd), ln_params[0], w_up[0], w_o.reshape(qd, d_model), w_down[0])
+        )(x_in.reshape(nc, rb, d_model), cos_full, sin_full, w_q.reshape(d_model, heads, hd), w_k[0], w_v[0], ln_params[0], w_up[0], w_o.reshape(qd, d_model), w_down[0])
         return out.reshape(1, num_micro, batch_dim, tok, d_model)
 
     in_specs = (P(None, "dp", "tp", None), P("pp", None, None), P("pp", None, "tp", None, None), P("pp", None, "tp", None), P("pp", None, "tp", None), P("pp", "tp", None, None, None), P("pp", None, "tp"), P("pp", "tp", None))

time: 858 us -> 851 us (level)
  no operation moved by 1% of the time
where the time goes in v5:
time: 851 us
  Pallas kernels  847 us (100%)
    pallas_call x1, Pallas kernels, stage_body(): pl.pallas_call(functools.partial(pipeline_kernel, (nc, LATE, tp, pp, head...  847 us

profile of v5, /device:TPU:1, one launch (start us, length us, event | category | flops | bytes accessed | tf_op | source)
XLA Modules:
  0.0 851.3 jit_solution(4030182565153871465)
XLA Ops:
  0.0 0.1 fusion.2
  0.2 0.7 pad_maximum_fusion
  0.9 847.0 %pipeline.1 = (bf16[64,32,2048]{2,1,0:T(8,128)(2,1)S(1)}, bf16[2048,512]{1,0:T(8,128)(2,1)}, bf16[2048,512]{1,0:T(8,128)(2,1)}, bf16[2048,512]{1,0:T(8,128)(2,1)...) custom-call(bf16[64,32,2048]{2,1,0:T(8,128)(2,1)} %bitcast.10, ...), custom_call_target="tpu_custom_call" | custom-call | flops 206158430208 | bytes 52428800 | tf_op jit(solution)/shard_map/pipeline/pallas_call | solution.py:390
  847.9 3.4 copy.10
  (1 shorter events, 0.0 us)

commit v6 on v5

--- a/solution.py
+++ b/solution.py
@@ -12,9 +12,10 @@
 CHUNKS_PER_MICRO = 8
 NT = 256
 NX, NR, NP, NS = 4, 4, 3, 4
-LATE = 3
+LATE = 4
+EARLY = 16
 AHEAD = 4
-TURN = (("gather0", 0), ("scatter1", 3), ("gather2", 1), ("up", 2), ("finish", 4), ("out", 2), ("scatter0", 2), ("lay_q", 0), ("gather1", 0), ("lay_k", 0), ("lay_v", 1), ("arrive", 1), ("scatter2", 3), ("heads", 1))
+TURN = (("gather0", 0), ("arrive", 2), ("scatter2", 4), ("heads", 2), ("gather2", 1), ("lay_v", 1), ("scatter1", 3), ("up", 2), ("lay_q", 0), ("gather1", 0), ("lay_k", 0), ("out", 2), ("scatter0", 2), ("finish", 4))
 MESH = pl.DeviceIdType.MESH
 
 
@@ -27,9 +28,9 @@
 
 def pipeline_kernel(dims, x_hbm, cos_tab, sin_tab, wq_hbm, wk_hbm, wv_hbm, ln_hbm, wup_hbm, wo_hbm, wdn_hbm,
                     xin, lq_hbm, lk_hbm, lv_hbm, lln_hbm, lup_hbm, lo_hbm, ldn_hbm,
-                    raw, wqkv, ln_ref, wup, wod, xlate, xfull, rbuf, part, ha, hm, qkv, act, mask_ref, cos_ref, sin_ref,
-                    w_sem, xin_sem, ag_ss, ag_rs, rs_ss, rs_rs, fwd_sem, home_sem, lw_ss, lw_rs):
-    nc, nl, tp, pp, heads, hd, tok = dims
+                    raw, wqkv, ln_ref, wup, wod, xlate, early, xfull, rbuf, part, ha, hm, qkv, act, mask_ref, cos_ref, sin_ref,
+                    w_sem, xin_sem, ag_ss, ag_rs, rs_ss, rs_rs, fwd_sem, home_sem, lw_ss, lw_rs, es_ss, es_rs, eh_ss, eh_rs):
+    nc, nl, ne, tp, pp, heads, hd, tok = dims
     rb, d_model = xin.shape[1:]
     rows = tp * rb
     ff = wup.shape[1]
@@ -94,11 +95,29 @@
     swap_copies = [pltpu.make_async_copy(src, dst, w_sem.at[k]) for k, (src, dst) in enumerate(zip(late, held))]
     lend_copies = [remote(src, dst, lw_ss.at[k], lw_rs.at[k], {"pp": jnp.maximum(s - half, 0)}) for k, (src, dst) in enumerate(zip(held[:3] + own[3:], late))]
 
+    helper = s == pp - 1
+
+    def other(j):
+        return lax.rem(z + j, tp)
+
+    def is_early(c):
+        return (s == 0) & (c >= 1) & (c <= ne)
+
+    def share_copy(c, j):
+        return remote(x_hbm.at[c], early.at[c - 1, z], es_ss.at[c - 1, j], es_rs.at[c - 1, z], {"tp": other(j)})
+
+    def got_copy(c, j):
+        return remote(x_hbm.at[c], early.at[c - 1, other(j)], es_ss.at[c - 1, j], es_rs.at[c - 1, other(j)], {"tp": other(j)})
+
+    def hand_copy(c, j):
+        b = other(j)
+        return remote(early.at[c - 1, b], early.at[c - 1, b], eh_ss.at[c - 1, b], eh_rs.at[c - 1, b], {"pp": 0})
+
     barrier = pltpu.get_barrier_semaphore()
-    for there, to in ((has_left, neighbour(1)), (has_right, neighbour(0)), (has_prev, {"pp": jnp.maximum(s - 1, 0)}), (has_next, {"pp": jnp.minimum(s + 1, pp - 1)}), (front, {"pp": jnp.minimum(s + half, pp - 1)}), (s >= half, {"pp": jnp.maximum(s - half, 0)})):
-        @pl.when(there)
-        def _(to=to):
-            pl.semaphore_signal(barrier, inc=1, device_id=to, device_id_type=MESH)
+    for j in range(1, tp):
+        pl.semaphore_signal(barrier, inc=1, device_id={"tp": other(j)}, device_id_type=MESH)
+    for j in range(1, pp):
+        pl.semaphore_signal(barrier, inc=1, device_id={"pp": lax.rem(s + j, pp)}, device_id_type=MESH)
 
     def load(c):
         return pltpu.make_async_copy(x_hbm.at[c], xin.at[c], xin_sem.at[c])
@@ -141,12 +160,27 @@
             cos_ref[to] = cos_tab[of]
             sin_ref[to] = sin_tab[of]
 
-    pl.semaphore_wait(barrier, has_left.astype(jnp.int32) + has_right.astype(jnp.int32) + has_prev.astype(jnp.int32) + has_next.astype(jnp.int32) + 1)
-
-    @pl.when(s >= half)
-    def _():
+    pl.semaphore_wait(barrier, tp - 1 + pp - 1)
+
+    def lend():
         for copy in lend_copies:
             copy.start()
+
+    @pl.when(helper)
+    def _():
+        def share(c, carry):
+            for j in range(1, tp):
+                share_copy(c, j).start()
+            return carry
+        lax.fori_loop(1, ne + 1, share, 0)
+
+        def hand(c, carry):
+            for j in range(1, tp):
+                got_copy(c, j).wait_recv()
+                hand_copy(c, j).start()
+            return carry
+        lax.fori_loop(1, ne + 1, hand, 0)
+        lend()
 
     def in_its_place(c, fn):
         on(c < nc, lambda: fn(xin.at[c]))
@@ -155,23 +189,35 @@
     def ag_start(c):
         on((s == 0) & (c + AHEAD < nc), lambda: load(c + AHEAD).start())
         pltpu.make_async_copy(x_hbm.at[0], xin.at[0], xin_sem.at[c]).wait()
+        on((s >= half) & ~helper & (c == 2), lend)
 
         def send(place):
             for way in (0, 1):
-                on(ag_sends(0, way), ag_copy(c, 0, way, place).start)
+                on(ag_sends(0, way) & ~is_early(c), ag_copy(c, 0, way, place).start)
             xfull[c % NX, z] = place[...]
         in_its_place(c, send)
 
     def ag_hop(c, h):
-        for way in (0, 1):
-            on(ag_gets(h - 1, way), ag_copy(c, h - 1, way).wait_recv)
-            if h < last:
-                on(ag_sends(h, way), ag_copy(c, h, way).start)
+        @pl.when(~is_early(c))
+        def _():
+            for way in (0, 1):
+                on(ag_gets(h - 1, way), ag_copy(c, h - 1, way).wait_recv)
+                if h < last:
+                    on(ag_sends(h, way), ag_copy(c, h, way).start)
+
+        if h == last:
+            @pl.when(is_early(c))
+            def _():
+                for j in range(1, tp):
+                    hand_copy(c, j).wait_recv()
+                    xfull[c % NX, other(j)] = early[c - 1, other(j)]
 
     def ag_drain(c):
-        for h in range(last):
-            for way in (0, 1):
-                on(ag_sends(h, way), ag_copy(c, h, way).wait_send)
+        @pl.when(~is_early(c))
+        def _():
+            for h in range(last):
+                for way in (0, 1):
+                    on(ag_sends(h, way), ag_copy(c, h, way).wait_send)
 
     def rs_hop(c, h):
         for way in (0, 1):
@@ -356,6 +402,15 @@
         on(s < half - 1, next_late_copy(nc + k).wait_send)
         on(front, home_copy(nc + k).wait_send)
 
+    @pl.when(helper)
+    def _():
+        def sent_early(c, carry):
+            for j in range(1, tp):
+                share_copy(c, j).wait_send()
+                hand_copy(c, j).wait_send()
+            return carry
+        lax.fori_loop(1, ne + 1, sent_early, 0)
+
     @pl.when(s >= half)
     def _():
         for copy in lend_copies:
@@ -388,7 +443,7 @@
         dma = pltpu.SemaphoreType.DMA
         flops = 2 * num_micro * tp * batch_dim * tok * (3 * qd * d_model + qd * d_model + 2 * ff * d_model)
         out, *_ = pl.pallas_call(
-            functools.partial(pipeline_kernel, (nc, LATE, tp, pp, heads, hd, tok)),
+            functools.partial(pipeline_kernel, (nc, LATE, EARLY, tp, pp, heads, hd, tok)),
             out_shape=[pltpu.VMEM((nc, rb, d_model), bf16)] + [jax.ShapeDtypeStruct((d_model, qd), bf16)] * 3 + [
                 jax.ShapeDtypeStruct((4, d_model), f32), jax.ShapeDtypeStruct((d_model, ff), bf16),
                 jax.ShapeDtypeStruct((qd, d_model), bf16), jax.ShapeDtypeStruct((ff, d_model), bf16)],
@@ -401,6 +456,7 @@
                 pltpu.VMEM((d_model, ff), bf16),
                 pltpu.VMEM((qd + ff, d_model), bf16),
                 pltpu.VMEM((LATE, rb, d_model), bf16),
+                pltpu.VMEM((EARLY, tp, rb, d_model), bf16),
                 pltpu.VMEM((NX, tp, rb, d_model), bf16),
                 pltpu.VMEM((NR, 2, tp - 1, rb, d_model), bf16),
                 pltpu.VMEM((NP, tp, rb, d_model), bf16),
@@ -421,6 +477,10 @@
                 dma((LATE,)),
                 dma((7,)),
                 dma((7,)),
+                dma((EARLY, tp)),
+                dma((EARLY, tp)),
+                dma((EARLY, tp)),
+                dma((EARLY, tp)),
             ],
             compiler_params=pltpu.CompilerParams(collective_id=0, has_side_effects=True, vmem_limit_bytes=52 * 2 ** 20),
             cost_estimate=pl.CostEstimate(flops=flops, bytes_accessed=50 * 2 ** 20, transcendentals=0),

time: 851 us -> 859 us (level)
  no operation moved by 1% of the time
where the time goes in v6:
time: 859 us; the launch traced here: 858 us
  Pallas kernels  854 us (99%)
    pallas_call x1, Pallas kernels, stage_body(): pl.pallas_call(functools.partial(pipeline_kernel, (nc, LATE, EARLY, tp, p...  854 us

profile of v6, /device:TPU:1, one launch (start us, length us, event | category | flops | bytes accessed | tf_op | source)
XLA Modules:
  0.0 858.4 jit_solution(9713036456188402524)
XLA Ops:
  0.0 0.1 fusion.2
  0.2 0.7 pad_maximum_fusion
  0.9 854.1 %pipeline.1 = (bf16[64,32,2048]{2,1,0:T(8,128)(2,1)S(1)}, bf16[2048,512]{1,0:T(8,128)(2,1)}, bf16[2048,512]{1,0:T(8,128)(2,1)}, bf16[2048,512]{1,0:T(8,128)(2,1)...) custom-call(bf16[64,32,2048]{2,1,0:T(8,128)(2,1)} %bitcast.10, ...), custom_call_target="tpu_custom_call" | custom-call | flops 206158430208 | bytes 52428800 | tf_op jit(solution)/shard_map/pipeline/pallas_call | solution.py:445
  855.0 3.4 copy.10
  (1 shorter events, 0.0 us)

commit v7 on v6

--- a/solution.py
+++ b/solution.py
@@ -12,10 +12,10 @@
 CHUNKS_PER_MICRO = 8
 NT = 256
 NX, NR, NP, NS = 4, 4, 3, 4
-LATE = 4
+LATE = 3
 EARLY = 16
 AHEAD = 4
-TURN = (("gather0", 0), ("arrive", 2), ("scatter2", 4), ("heads", 2), ("gather2", 1), ("lay_v", 1), ("scatter1", 3), ("up", 2), ("lay_q", 0), ("gather1", 0), ("lay_k", 0), ("out", 2), ("scatter0", 2), ("finish", 4))
+TURN = (("gather0", 0), ("scatter1", 3), ("gather2", 1), ("up", 2), ("finish", 4), ("out", 2), ("scatter0", 2), ("lay_q", 0), ("gather1", 0), ("lay_k", 0), ("lay_v", 1), ("arrive", 1), ("scatter2", 3), ("heads", 1))
 MESH = pl.DeviceIdType.MESH
 
 
@@ -97,25 +97,32 @@
 
     helper = s == pp - 1
 
-    def other(j):
-        return lax.rem(z + j, tp)
-
     def is_early(c):
         return (s == 0) & (c >= 1) & (c <= ne)
 
-    def share_copy(c, j):
-        return remote(x_hbm.at[c], early.at[c - 1, z], es_ss.at[c - 1, j], es_rs.at[c - 1, z], {"tp": other(j)})
-
-    def got_copy(c, j):
-        return remote(x_hbm.at[c], early.at[c - 1, other(j)], es_ss.at[c - 1, j], es_rs.at[c - 1, other(j)], {"tp": other(j)})
-
-    def hand_copy(c, j):
-        b = other(j)
+    def share_copy(c, h, way):
+        b = jnp.clip(z - h if way == 0 else z + h, 0, last)
+        src = x_hbm.at[c] if h == 0 else early.at[c - 1, b]
+        return remote(src, early.at[c - 1, b], es_ss.at[c - 1, way, h], es_rs.at[c - 1, way, h], neighbour(way))
+
+    def hand_copy(c, b):
         return remote(early.at[c - 1, b], early.at[c - 1, b], eh_ss.at[c - 1, b], eh_rs.at[c - 1, b], {"pp": 0})
+
+    def share_hop(c, h):
+        for way in (0, 1):
+            if h > 0:
+                @pl.when(ag_gets(h - 1, way))
+                def _(way=way):
+                    share_copy(c, h - 1, way).wait_recv()
+                    if h < last:
+                        on(ag_sends(h, way), share_copy(c, h, way).start)
+                    hand_copy(c, z - h if way == 0 else z + h).start()
+            else:
+                on(ag_sends(0, way), share_copy(c, 0, way).start)
 
     barrier = pltpu.get_barrier_semaphore()
     for j in range(1, tp):
-        pl.semaphore_signal(barrier, inc=1, device_id={"tp": other(j)}, device_id_type=MESH)
+        pl.semaphore_signal(barrier, inc=1, device_id={"tp": lax.rem(z + j, tp)}, device_id_type=MESH)
     for j in range(1, pp):
         pl.semaphore_signal(barrier, inc=1, device_id={"pp": lax.rem(s + j, pp)}, device_id_type=MESH)
 
@@ -168,18 +175,11 @@
 
     @pl.when(helper)
     def _():
-        def share(c, carry):
-            for j in range(1, tp):
-                share_copy(c, j).start()
-            return carry
-        lax.fori_loop(1, ne + 1, share, 0)
-
-        def hand(c, carry):
-            for j in range(1, tp):
-                got_copy(c, j).wait_recv()
-                hand_copy(c, j).start()
-            return carry
-        lax.fori_loop(1, ne + 1, hand, 0)
+        def share(i, carry):
+            for h in range(tp):
+                on((i - h >= 1) & (i - h <= ne), functools.partial(share_hop, i - h, h))
+            return carry
+        lax.fori_loop(1, ne + tp, share, 0)
         lend()
 
     def in_its_place(c, fn):
@@ -209,8 +209,9 @@
             @pl.when(is_early(c))
             def _():
                 for j in range(1, tp):
-                    hand_copy(c, j).wait_recv()
-                    xfull[c % NX, other(j)] = early[c - 1, other(j)]
+                    b = lax.rem(z + j, tp)
+                    hand_copy(c, b).wait_recv()
+                    xfull[c % NX, b] = early[c - 1, b]
 
     def ag_drain(c):
         @pl.when(~is_early(c))
@@ -405,9 +406,11 @@
     @pl.when(helper)
     def _():
         def sent_early(c, carry):
+            for h in range(last):
+                for way in (0, 1):
+                    on(ag_sends(h, way), share_copy(c, h, way).wait_send)
             for j in range(1, tp):
-                share_copy(c, j).wait_send()
-                hand_copy(c, j).wait_send()
+                hand_copy(c, lax.rem(z + j, tp)).wait_send()
             return carry
         lax.fori_loop(1, ne + 1, sent_early, 0)
 
@@ -477,8 +480,8 @@
                 dma((LATE,)),
                 dma((7,)),
                 dma((7,)),
-                dma((EARLY, tp)),
-                dma((EARLY, tp)),
+                dma((EARLY, 2, tp - 1)),
+                dma((EARLY, 2, tp - 1)),
                 dma((EARLY, tp)),
                 dma((EARLY, tp)),
             ],

time: 859 us -> 839 us (0.977)
  Pallas kernels: 854 us -> 834 us
    pallas_call x1, Pallas kernels: 854 us -> 834 us  [stage_body(): pl.pallas_call(functools.partial(pipeline_kernel, (nc, LATE, EARLY, tp, p...]
where the time goes in v7:
time: 839 us
  Pallas kernels  834 us (99%)
    pallas_call x1, Pallas kernels, stage_body(): pl.pallas_call(functools.partial(pipeline_kernel, (nc, LATE, EARLY, tp, p...  834 us

profile of v7, /device:TPU:1, one launch (start us, length us, event | category | flops | bytes accessed | tf_op | source)
XLA Modules:
  0.0 838.6 jit_solution(3692965158497269233)
XLA Ops:
  0.0 0.1 fusion.2
  0.2 0.7 pad_maximum_fusion
  0.9 834.4 %pipeline.1 = (bf16[64,32,2048]{2,1,0:T(8,128)(2,1)S(1)}, bf16[2048,512]{1,0:T(8,128)(2,1)}, bf16[2048,512]{1,0:T(8,128)(2,1)}, bf16[2048,512]{1,0:T(8,128)(2,1)...) custom-call(bf16[64,32,2048]{2,1,0:T(8,128)(2,1)} %bitcast.10, ...), custom_call_target="tpu_custom_call" | custom-call | flops 206158430208 | bytes 52428800 | tf_op jit(solution)/shard_map/pipeline/pallas_call | solution.py:448
  835.2 3.4 copy.10
  (1 shorter events, 0.0 us)

commit v8 on v7

--- a/solution.py
+++ b/solution.py
@@ -12,10 +12,10 @@
 CHUNKS_PER_MICRO = 8
 NT = 256
 NX, NR, NP, NS = 4, 4, 3, 4
-LATE = 3
-EARLY = 16
+LATE = 5
+EARLY = 24
 AHEAD = 4
-TURN = (("gather0", 0), ("scatter1", 3), ("gather2", 1), ("up", 2), ("finish", 4), ("out", 2), ("scatter0", 2), ("lay_q", 0), ("gather1", 0), ("lay_k", 0), ("lay_v", 1), ("arrive", 1), ("scatter2", 3), ("heads", 1))
+TURN = (("gather0", 0), ("arrive", 2), ("scatter2", 4), ("heads", 2), ("gather2", 1), ("lay_v", 1), ("scatter1", 3), ("up", 2), ("lay_q", 0), ("gather1", 0), ("lay_k", 0), ("out", 2), ("scatter0", 2), ("finish", 4))
 MESH = pl.DeviceIdType.MESH
 
 
@@ -485,7 +485,7 @@
                 dma((EARLY, tp)),
                 dma((EARLY, tp)),
             ],
-            compiler_params=pltpu.CompilerParams(collective_id=0, has_side_effects=True, vmem_limit_bytes=52 * 2 ** 20),
+            compiler_params=pltpu.CompilerParams(collective_id=0, has_side_effects=True, vmem_limit_bytes=54 * 2 ** 20),
             cost_estimate=pl.CostEstimate(flops=flops, bytes_accessed=50 * 2 ** 20, transcendentals=0),
             name="pipeline",
         )(x_in.reshape(nc, rb, d_model), cos_full, sin_full, w_q.reshape(d_model, heads, hd), w_k[0], w_v[0], ln_params[0], w_up[0], w_o.reshape(qd, d_model), w_down[0])

time: 839 us -> 851 us (1.014)
  Pallas kernels: 834 us -> 846 us
    pallas_call x1, Pallas kernels: 834 us -> 846 us  [stage_body(): pl.pallas_call(functools.partial(pipeline_kernel, (nc, LATE, EARLY, tp, p...]
where the time goes in v8:
time: 851 us; the launch traced here: 850 us
  Pallas kernels  846 us (99%)
    pallas_call x1, Pallas kernels, stage_body(): pl.pallas_call(functools.partial(pipeline_kernel, (nc, LATE, EARLY, tp, p...  846 us

profile of v8, /device:TPU:1, one launch (start us, length us, event | category | flops | bytes accessed | tf_op | source)
XLA Modules:
  0.0 850.0 jit_solution(5442570635718404663)
XLA Ops:
  0.0 0.1 fusion.2
  0.2 0.7 pad_maximum_fusion
  0.9 845.8 %pipeline.1 = (bf16[64,32,2048]{2,1,0:T(8,128)(2,1)S(1)}, bf16[2048,512]{1,0:T(8,128)(2,1)}, bf16[2048,512]{1,0:T(8,128)(2,1)}, bf16[2048,512]{1,0:T(8,128)(2,1)...) custom-call(bf16[64,32,2048]{2,1,0:T(8,128)(2,1)} %bitcast.10, ...), custom_call_target="tpu_custom_call" | custom-call | flops 206158430208 | bytes 52428800 | tf_op jit(solution)/shard_map/pipeline/pallas_call | solution.py:448
  846.6 3.4 copy.10
  (1 shorter events, 0.0 us)

commit v9 on v8

--- a/solution.py
+++ b/solution.py
@@ -12,10 +12,11 @@
 CHUNKS_PER_MICRO = 8
 NT = 256
 NX, NR, NP, NS = 4, 4, 3, 4
-LATE = 5
+LATE = 4
 EARLY = 24
+LEND_AT = 8
 AHEAD = 4
-TURN = (("gather0", 0), ("arrive", 2), ("scatter2", 4), ("heads", 2), ("gather2", 1), ("lay_v", 1), ("scatter1", 3), ("up", 2), ("lay_q", 0), ("gather1", 0), ("lay_k", 0), ("out", 2), ("scatter0", 2), ("finish", 4))
+TURN = (("gather0", 0), ("scatter1", 3), ("gather2", 1), ("up", 2), ("finish", 4), ("out", 2), ("scatter0", 2), ("lay_q", 0), ("gather1", 0), ("lay_k", 0), ("lay_v", 1), ("arrive", 1), ("scatter2", 3), ("heads", 1))
 MESH = pl.DeviceIdType.MESH
 
 
@@ -180,7 +181,6 @@
                 on((i - h >= 1) & (i - h <= ne), functools.partial(share_hop, i - h, h))
             return carry
         lax.fori_loop(1, ne + tp, share, 0)
-        lend()
 
     def in_its_place(c, fn):
         on(c < nc, lambda: fn(xin.at[c]))
@@ -189,7 +189,7 @@
     def ag_start(c):
         on((s == 0) & (c + AHEAD < nc), lambda: load(c + AHEAD).start())
         pltpu.make_async_copy(x_hbm.at[0], xin.at[0], xin_sem.at[c]).wait()
-        on((s >= half) & ~helper & (c == 2), lend)
+        on((s >= half) & (c == LEND_AT), lend)
 
         def send(place):
             for way in (0, 1):

time: 851 us -> 834 us (0.980)
  Pallas kernels: 846 us -> 829 us
    pallas_call x1, Pallas kernels: 846 us -> 829 us  [stage_body(): pl.pallas_call(functools.partial(pipeline_kernel, (nc, LATE, EARLY, tp, p...]
where the time goes in v9:
time: 834 us
  Pallas kernels  829 us (99%)
    pallas_call x1, Pallas kernels, stage_body(): pl.pallas_call(functools.partial(pipeline_kernel, (nc, LATE, EARLY, tp, p...  829 us

profile of v9, /device:TPU:1, one launch (start us, length us, event | category | flops | bytes accessed | tf_op | source)
XLA Modules:
  0.0 833.7 jit_solution(14806050269871157843)
XLA Ops:
  0.0 0.1 fusion.2
  0.2 0.7 pad_maximum_fusion
  0.9 829.4 %pipeline.1 = (bf16[64,32,2048]{2,1,0:T(8,128)(2,1)S(1)}, bf16[2048,512]{1,0:T(8,128)(2,1)}, bf16[2048,512]{1,0:T(8,128)(2,1)}, bf16[2048,512]{1,0:T(8,128)(2,1)...) custom-call(bf16[64,32,2048]{2,1,0:T(8,128)(2,1)} %bitcast.10, ...), custom_call_target="tpu_custom_call" | custom-call | flops 206158430208 | bytes 52428800 | tf_op jit(solution)/shard_map/pipeline/pallas_call | solution.py:448
  830.3 3.4 copy.10
  (1 shorter events, 0.0 us)

commit v10 on v8

--- a/solution.py
+++ b/solution.py
@@ -14,6 +14,7 @@
 NX, NR, NP, NS = 4, 4, 3, 4
 LATE = 5
 EARLY = 24
+LEND_AT = (5, 12)
 AHEAD = 4
 TURN = (("gather0", 0), ("arrive", 2), ("scatter2", 4), ("heads", 2), ("gather2", 1), ("lay_v", 1), ("scatter1", 3), ("up", 2), ("lay_q", 0), ("gather1", 0), ("lay_k", 0), ("out", 2), ("scatter0", 2), ("finish", 4))
 MESH = pl.DeviceIdType.MESH
@@ -180,7 +181,6 @@
                 on((i - h >= 1) & (i - h <= ne), functools.partial(share_hop, i - h, h))
             return carry
         lax.fori_loop(1, ne + tp, share, 0)
-        lend()
 
     def in_its_place(c, fn):
         on(c < nc, lambda: fn(xin.at[c]))
@@ -189,7 +189,8 @@
     def ag_start(c):
         on((s == 0) & (c + AHEAD < nc), lambda: load(c + AHEAD).start())
         pltpu.make_async_copy(x_hbm.at[0], xin.at[0], xin_sem.at[c]).wait()
-        on((s >= half) & ~helper & (c == 2), lend)
+        for k in range(half):
+            on((s == half + k) & (c == LEND_AT[k]), lend)
 
         def send(place):
             for way in (0, 1):

time: 851 us -> 851 us (level)
  no operation moved by 1% of the time
where the time goes in v10:
time: 851 us
  Pallas kernels  846 us (99%)
    pallas_call x1, Pallas kernels, stage_body(): pl.pallas_call(functools.partial(pipeline_kernel, (nc, LATE, EARLY, tp, p...  846 us

profile of v10, /device:TPU:1, one launch (start us, length us, event | category | flops | bytes accessed | tf_op | source)
XLA Modules:
  0.0 850.5 jit_solution(13789179025010142752)
XLA Ops:
  0.0 0.1 fusion.2
  0.2 0.7 pad_maximum_fusion
  0.9 846.2 %pipeline.1 = (bf16[64,32,2048]{2,1,0:T(8,128)(2,1)S(1)}, bf16[2048,512]{1,0:T(8,128)(2,1)}, bf16[2048,512]{1,0:T(8,128)(2,1)}, bf16[2048,512]{1,0:T(8,128)(2,1)...) custom-call(bf16[64,32,2048]{2,1,0:T(8,128)(2,1)} %bitcast.10, ...), custom_call_target="tpu_custom_call" | custom-call | flops 206158430208 | bytes 52428800 | tf_op jit(solution)/shard_map/pipeline/pallas_call | solution.py:449
  847.1 3.4 copy.10
  (1 shorter events, 0.0 us)

commit v11 on v10

--- a/solution.py
+++ b/solution.py
@@ -12,11 +12,11 @@
 CHUNKS_PER_MICRO = 8
 NT = 256
 NX, NR, NP, NS = 4, 4, 3, 4
-LATE = 5
+LATE = 4
 EARLY = 24
 LEND_AT = (5, 12)
 AHEAD = 4
-TURN = (("gather0", 0), ("arrive", 2), ("scatter2", 4), ("heads", 2), ("gather2", 1), ("lay_v", 1), ("scatter1", 3), ("up", 2), ("lay_q", 0), ("gather1", 0), ("lay_k", 0), ("out", 2), ("scatter0", 2), ("finish", 4))
+TURN = (("gather0", 0), ("scatter1", 3), ("gather2", 1), ("up", 2), ("finish", 4), ("out", 2), ("scatter0", 2), ("lay_q", 0), ("gather1", 0), ("lay_k", 0), ("lay_v", 1), ("arrive", 1), ("scatter2", 3), ("heads", 1))
 MESH = pl.DeviceIdType.MESH
 
 

time: 851 us -> 835 us (0.981)
  Pallas kernels: 846 us -> 831 us
    pallas_call x1, Pallas kernels: 846 us -> 831 us  [stage_body(): pl.pallas_call(functools.partial(pipeline_kernel, (nc, LATE, EARLY, tp, p...]
where the time goes in v11:
time: 835 us
  Pallas kernels  831 us (100%)
    pallas_call x1, Pallas kernels, stage_body(): pl.pallas_call(functools.partial(pipeline_kernel, (nc, LATE, EARLY, tp, p...  831 us

profile of v11, /device:TPU:1, one launch (start us, length us, event | category | flops | bytes accessed | tf_op | source)
XLA Modules:
  0.0 835.2 jit_solution(3947057669163173644)
XLA Ops:
  0.0 0.1 fusion.2
  0.2 0.7 pad_maximum_fusion
  0.9 830.9 %pipeline.1 = (bf16[64,32,2048]{2,1,0:T(8,128)(2,1)S(1)}, bf16[2048,512]{1,0:T(8,128)(2,1)}, bf16[2048,512]{1,0:T(8,128)(2,1)}, bf16[2048,512]{1,0:T(8,128)(2,1)...) custom-call(bf16[64,32,2048]{2,1,0:T(8,128)(2,1)} %bitcast.10, ...), custom_call_target="tpu_custom_call" | custom-call | flops 206158430208 | bytes 52428800 | tf_op jit(solution)/shard_map/pipeline/pallas_call | solution.py:449
  831.8 3.4 copy.10
  (1 shorter events, 0.0 us)

commit v12 on v9

--- a/solution.py
+++ b/solution.py
@@ -13,10 +13,10 @@
 NT = 256
 NX, NR, NP, NS = 4, 4, 3, 4
 LATE = 4
-EARLY = 24
+EARLY = 22
 LEND_AT = 8
 AHEAD = 4
-TURN = (("gather0", 0), ("scatter1", 3), ("gather2", 1), ("up", 2), ("finish", 4), ("out", 2), ("scatter0", 2), ("lay_q", 0), ("gather1", 0), ("lay_k", 0), ("lay_v", 1), ("arrive", 1), ("scatter2", 3), ("heads", 1))
+TURN = (("gather0", 0), ("scatter1", 3), ("gather2", 1), ("up", 2), ("finish", 4), ("out", 2), ("lay_q", 0), ("gather1", 0), ("lay_k", 0), ("scatter0", 2), ("scatter2", 3), ("lay_v", 1), ("arrive", 1), ("heads", 1))
 MESH = pl.DeviceIdType.MESH
 
 

time: 834 us -> 835 us (level)
  no operation moved by 1% of the time
where the time goes in v12:
time: 835 us
  Pallas kernels  831 us (100%)
    pallas_call x1, Pallas kernels, stage_body(): pl.pallas_call(functools.partial(pipeline_kernel, (nc, LATE, EARLY, tp, p...  831 us

profile of v12, /device:TPU:1, one launch (start us, length us, event | category | flops | bytes accessed | tf_op | source)
XLA Modules:
  0.0 835.1 jit_solution(2550390333261685692)
XLA Ops:
  0.0 0.1 fusion.2
  0.2 0.7 pad_maximum_fusion
  0.9 830.8 %pipeline.1 = (bf16[64,32,2048]{2,1,0:T(8,128)(2,1)S(1)}, bf16[2048,512]{1,0:T(8,128)(2,1)}, bf16[2048,512]{1,0:T(8,128)(2,1)}, bf16[2048,512]{1,0:T(8,128)(2,1)...) custom-call(bf16[64,32,2048]{2,1,0:T(8,128)(2,1)} %bitcast.10, ...), custom_call_target="tpu_custom_call" | custom-call | flops 206158430208 | bytes 52428800 | tf_op jit(solution)/shard_map/pipeline/pallas_call | solution.py:448
  831.7 3.4 copy.10
  (1 shorter events, 0.0 us)
